TPU v7x, 512 devices: a whole 4x4x16 slice. The times are simulated.
512 devices in a mesh: gx: 8 (over z_hi, x), gy: 8 (over y, core), gz: 8 (over z_lo).
Axes of the slice: x: 4, y: 4, z: 16 (z_hi: 2, z_lo: 8; z = z_hi * 8 + z_lo), core: 2. Of those that a mesh axis runs over, the one named last changes fastest.
Arguments:
- grains: float32 [12, 64, 128, 1024], P(None, 'gz', 'gx', 'gy'), may hold values from 0 to 0.6
- solute: float32 [64, 128, 1024], P('gz', 'gx', 'gy'), may hold values from 0 to 0.6
- thermal: float32 [8, 8, 8, 40, 4096], P('gz', 'gx', 'gy'), may hold values from 0.5 to 1.5
- block_slot: int32 [8, 8, 8, 20], P('gz', 'gx', 'gy'), may hold values from -1 to 39, as said below
- block_owner: int32 [8, 8, 8, 20], P('gz', 'gx', 'gy'), may hold values from -1 to 7, as said below
- block_offset: int32 [8, 8, 8, 3, 20], P('gz', 'gx', 'gy'), may hold values from -31 to 128, as said below
Outputs:
- grains_out: float32 [12, 64, 128, 1024], P(None, 'gz', 'gx', 'gy')
- solute_out: float32 [64, 128, 1024], P('gz', 'gx', 'gy')
- temperature: float32 [64, 128, 1024], P('gz', 'gx', 'gy')
Inputs may be any that keep to these rules, and one draw needn't show every extreme that they name: `block_slot`: -1 exactly where block_owner is -1; the live entries of all tiles name distinct pairs (owner, slot) within a column. `block_owner`: -1 marks an empty entry. No owner serves more than 5 live entries of one tile; in every draw, in each column, some owner serves 5 entries of every tile of that column; and in every draw some tile of the box has all 20 entries live. `block_offset`: 0 for empty entries. Along each dimension the live starts of a tile differ by multiples of 32, and the hats of a tile's live blocks sum to one at each of its cells.
All inputs are finite; a program needn't handle non-finite values.
Results may differ from a plain program's by a relative error of at most 0.0003.
Values sent between devices are 32-bit elements; how exact they have to be, the bound alone decides.
A program may use at most 64 MiB of HBM per device.

v0:
```python
import math

import jax
import jax.numpy as jnp
from jax import lax
from jax.sharding import PartitionSpec as P

BLOCK = 16
STEPS = 3


step_rate = 0.1
stiffness = 1.6
cross_energy = 0.25
drive_scale = 2.0
liquidus_slope = 0.5
rejection = 0.5
diffusion_rate = 0.15


def side_by_side(arrays, axis, split_dim, concat_dim, along):
    widths = [math.prod(a.shape[along:]) for a in arrays]
    both = jnp.concatenate(
        [a.reshape(*a.shape[:along], w) for a, w in zip(arrays, widths)], axis=along
    )
    filled = lax.all_to_all(both, axis, split_axis=split_dim, concat_axis=concat_dim, tiled=True)
    pieces = jnp.split(filled, [sum(widths[:k]) for k in range(1, len(widths))], axis=along)
    return tuple(
        (b.reshape(*filled.shape[:along], *a.shape[along:]) for a, b in zip(arrays, pieces))
    )


def with_halo(cells, sides, width):
    for axis, dim in sides:
        count = lax.axis_size(axis)
        head = lax.slice_in_dim(cells, 0, width, axis=dim)
        tail = lax.slice_in_dim(cells, cells.shape[dim] - width, cells.shape[dim], axis=dim)
        cells = jnp.concatenate(
            [
                lax.ppermute(tail, axis, [(i, (i + 1) % count) for i in range(count)]),
                cells,
                lax.ppermute(head, axis, [((i + 1) % count, i) for i in range(count)]),
            ],
            axis=dim,
        )
    return cells


def hat_weights(starts, cell_count):
    positions = jnp.arange(cell_count, dtype=jnp.float32)
    node_sites = 2.0 * jnp.arange(BLOCK, dtype=jnp.float32)
    distance = (
        positions[None, :, None]
        - starts.astype(jnp.float32)[:, None, None]
        - node_sites[None, None, :]
    )
    return jnp.maximum(0.0, 1.0 - jnp.abs(distance) / 2.0)


def project(blocks, starts, live_entry, layers, breadth, length):
    entries = blocks.shape[0]
    cubes = blocks.reshape(entries, BLOCK, BLOCK, BLOCK)
    weight_z = hat_weights(starts[0], layers) * live_entry.astype(jnp.float32)[:, None, None]
    weight_x = hat_weights(starts[1], breadth)
    weight_y = hat_weights(starts[2], length)
    along_y = jnp.einsum("epqr,eyr->epqy", cubes, weight_y, precision=lax.Precision.HIGHEST)
    along_x = jnp.einsum("exq,epqy->epxy", weight_x, along_y, precision=lax.Precision.HIGHEST)
    return (weight_z, along_x)


def laplace(padded):
    middle = padded[..., 1:-1, 1:-1, 1:-1]
    return (
        padded[..., 2:, 1:-1, 1:-1]
        + padded[..., :-2, 1:-1, 1:-1]
        + padded[..., 1:-1, 2:, 1:-1]
        + padded[..., 1:-1, :-2, 1:-1]
        + padded[..., 1:-1, 1:-1, 2:]
        + padded[..., 1:-1, 1:-1, :-2]
        - 6.0 * middle
    )


def advance(padded, heat_field):
    orders = padded[:-1]
    concentration = padded[-1]
    squares = jnp.sum(orders * orders, axis=0)
    bending = laplace(orders)
    diffusion_term = laplace(concentration - rejection * squares)
    central = orders[:, 1:-1, 1:-1, 1:-1]
    central_sum = squares[1:-1, 1:-1, 1:-1]
    central_solute = concentration[1:-1, 1:-1, 1:-1]
    undercool = drive_scale * (1.0 - heat_field - liquidus_slope * central_solute)
    double_well = 2.0 * central * (1.0 - central) * (1.0 - 2.0 * central)
    contact_term = 4.0 * cross_energy * central * (central_sum - central * central)
    growth_term = 30.0 * central * central * (1.0 - central) * (1.0 - central) * undercool
    new_orders = central + step_rate * (
        stiffness * bending - double_well - contact_term + growth_term
    )
    new_solute = central_solute + diffusion_rate * diffusion_term
    return jnp.concatenate([new_orders, new_solute[None]], axis=0)


def reflect(padded, margin):
    at_bottom = lax.axis_index("gz") == 0
    at_top = lax.axis_index("gz") == lax.axis_size("gz") - 1
    length = padded.shape[1]
    mirror_low = jnp.flip(padded[:, margin : 2 * margin], axis=1)
    mirror_high = jnp.flip(padded[:, length - 2 * margin : length - margin], axis=1)
    low_part = jnp.where(at_bottom, mirror_low, padded[:, :margin])
    high_part = jnp.where(at_top, mirror_high, padded[:, length - margin :])
    return jnp.concatenate([low_part, padded[:, margin : length - margin], high_part], axis=1)


def trim(source, amount):
    return source[amount:-amount, amount:-amount, amount:-amount]


def body(grains, solute, thermal, block_slot, block_owner, block_offset):
    owners = lax.axis_size("gz")
    stored = thermal.reshape(thermal.shape[3], thermal.shape[4])
    capacity = stored.shape[0] // owners
    slot_ids = block_slot.reshape(-1)
    holders = block_owner.reshape(-1)
    starts = block_offset.reshape(3, -1)
    entries = slot_ids.shape[0]
    live_entry = holders >= 0
    entry_index = jnp.arange(entries, dtype=jnp.int32)
    earlier = (holders[:, None] == holders[None, :]) & (entry_index[None, :] < entry_index[:, None])
    before = jnp.sum(earlier.astype(jnp.int32), axis=1)
    position = holders * capacity + before
    places = jnp.arange(owners * capacity, dtype=jnp.int32)
    routing = ((position[:, None] == places[None, :]) & live_entry[:, None]).astype(jnp.int32)
    wanted = (jnp.sum(routing * (slot_ids[:, None] + 1), axis=0) - 1).reshape(owners, capacity)
    layers, breadth, length = solute.shape
    wanted_start = jnp.sum(starts[:, :, None] * routing[None, :, :], axis=1)
    wanted_start = jnp.transpose(wanted_start.reshape(3, owners, capacity), (1, 0, 2))
    requested, requested_start = side_by_side((wanted, wanted_start), "gz", 0, 0, 1)
    requested_flat = requested.reshape(-1)
    picked = stored[jnp.clip(requested_flat, 0, stored.shape[0] - 1)]
    flat_start = jnp.transpose(requested_start, (1, 0, 2)).reshape(3, -1)
    weight_z, along_x = project(picked, flat_start, requested_flat >= 0, layers, breadth, length)
    weight_z = weight_z.reshape(owners, capacity, layers, BLOCK)
    along_x = along_x.reshape(owners, capacity, BLOCK, breadth, length)
    regions = jnp.einsum("gkzp,gkpxy->gzxy", weight_z, along_x, precision=lax.Precision.HIGHEST)
    returned = lax.all_to_all(regions, "gz", split_axis=0, concat_axis=0, tiled=True)
    heat_field = jnp.sum(returned, axis=0)
    fields = jnp.concatenate([grains, solute[None]], axis=0)
    stacked = jnp.concatenate([fields, heat_field[None]], axis=0)
    padded = with_halo(stacked, (("gx", 2), ("gy", 3), ("gz", 1)), STEPS)
    padded = reflect(padded, STEPS)
    fields = padded[:-1]
    warmth = padded[-1]
    for repeat in range(STEPS):
        fields = advance(fields, trim(warmth, repeat + 1))
    return (fields[:-1], fields[-1], heat_field)


def solution(mesh):
    in_specs = (
        P(None, "gz", "gx", "gy"),
        P("gz", "gx", "gy"),
        P("gz", "gx", "gy", None, None),
        P("gz", "gx", "gy", None),
        P("gz", "gx", "gy", None),
        P("gz", "gx", "gy", None, None),
    )
    out_specs = (P(None, "gz", "gx", "gy"), P("gz", "gx", "gy"), P("gz", "gx", "gy"))
    return jax.shard_map(body, mesh=mesh, in_specs=in_specs, out_specs=out_specs, check_vma=False)
```

profile of v0, /device:TPU:15, one launch (start us, length us, event | category | flops | bytes accessed | tf_op | source)
XLA Modules:
  0.0 214.4 jit_solution(9481014492807088315)
XLA Ops:
  5.5 12.2 %all-to-all-start = ((s32[8,1,20]{2,1,0:T(1,128)}), s32[8,1,20]{2,1,0:T(1,128)S(1)}, u32[]{:S(2)}, u32[]{:S(2)}) async-start(s32[8,1,20]{2,1,0:T(1,128)} %bitcast.4), calls=%async_computation | async-start | bytes 8192 | tf_op jit(solution)/shard_map/all_to_all | solution.py:26
  17.7 9.2 %all-to-all-done = s32[8,1,20]{2,1,0:T(1,128)S(1)} async-done(((s32[8,1,20]{2,1,0:T(1,128)}), s32[8,1,20]{2,1,0:T(1,128)S(1)}, u32[]{:S(2)}, u32[]{:S(2)}) %all-to-all-start) | async-done | bytes 672 | tf_op jit(solution)/shard_map/all_to_all | solution.py:26
  29.2 5.6 %copy.69 = f32[40,16,16,16]{3,2,1,0:T(8,128)} copy(f32[40,16,16,16]{0,3,2,1:T(8,128)S(1)} %bitcast.54) | data formatting | bytes 1310720 | tf_op jit(solution)/shard_map/reshape | solution.py:62
  34.8 7.0 %fusion.32 = f32[40,16,16,128]{3,2,1,0:T(8,128)S(1)} fusion(f32[40,16,16,16]{3,2,1,0:T(8,128)} %copy.69, f32[16]{0:T(128)S(1)} %iota_multiply_fusion, f32[40,128]{1,0:T(8,128)S(1)} %iota_subtract_fusion.2), kind=kOutput, calls=%fused_computation.65 | convolution fusion | flops 252067840 | bytes 5918784 | tf_op jit(solution)/shard_map/epqr,eyr->epqy/dot_general | solution.py:66
  41.8 5.0 %fusion.30 = f32[40,16,128,16]{2,3,1,0:T(8,128)S(1)} fusion(f32[40,16,16,128]{3,2,1,0:T(8,128)S(1)} %fusion.32, f32[16]{0:T(128)S(1)} %iota_multiply_fusion, f32[40,16]{1,0:T(8,128)S(1)} %iota_subtract_fusion.1), kind=kOutput, calls=%fused_computation.63 | convolution fusion | flops 251709440 | bytes 10488384 | tf_op jit(solution)/shard_map/exq,epqy->epxy/dot_general | solution.py:67
  46.8 7.5 %fusion.19 = f32[8,8,16,128]{3,1,2,0:T(8,128)} fusion(f32[8,5,16,16,128]{4,3,2,1,0:T(8,128)S(1)} %bitcast.53, f32[8,5]{1,0:T(8,128)S(1)} %compare_convert_fusion, f32[16]{0:T(128)S(1)} %iota_multiply_fusion, f32[8,5,8]{2,1,0:T(8,128)S(1)} %iota_subtract_fusion), kind=kOutput, calls=%fused_computation.42 | convolution fusion | flops 125859840 | bytes 5768672 | tf_op jit(solution)/shard_map/gkzp,gkpxy->gzxy/dot_general | solution.py:145
  54.3 3.5 %all-to-all-start.1 = ((f32[8,8,16,128]{3,1,2,0:T(8,128)}), f32[8,8,16,128]{3,1,2,0:T(8,128)S(1)}, u32[]{:S(2)}, u32[]{:S(2)}) async-start(f32[8,8,16,128]{3,1,2,0:T(8,128)} %fusion.19), calls=%async_computation.1 | async-start | bytes 1048576 | tf_op jit(solution)/shard_map/all_to_all | solution.py:146
  58.1 20.4 %all-to-all-done.1 = f32[8,8,16,128]{3,1,2,0:T(8,128)S(1)} async-done(((f32[8,8,16,128]{3,1,2,0:T(8,128)}), f32[8,8,16,128]{3,1,2,0:T(8,128)S(1)}, u32[]{:S(2)}, u32[]{:S(2)}) %all-to-all-start.1) | async-done | bytes 524320 | tf_op jit(solution)/shard_map/all_to_all | solution.py:146
  78.6 7.9 %collective-permute-start = (f32[14,8,3,128]{3,1,2,0:T(8,128)S(1)}, f32[14,8,3,128]{3,1,2,0:T(8,128)S(1)}, u32[]{:S(2)}, u32[]{:S(2)}) collective-permute-start(f32[14,8,3,128]{3,1,2,0:T(8,128)S(1)} %get-tuple-element.26), channel_id=1, source_target_pairs={{0,64},{64,128},{128,192},{192,256},{256,320},{320,384},{384,448},... | collective-permute-start | bytes 516104 | tf_op jit(solution)/shard_map/ppermute | solution.py:40
  86.4 2.1 collective-permute-start.1
  88.8 14.8 %collective-permute-done.1 = f32[14,8,3,128]{3,1,2,0:T(8,128)S(1)} collective-permute-done((f32[14,8,3,128]{3,1,2,0:T(8,128)S(1)}, f32[14,8,3,128]{3,1,2,0:T(8,128)S(1)}, u32[]{:S(2)}, u32[]{:S(2)}) %collective-permute-start.1) | collective-permute-done | bytes 172064 | tf_op jit(solution)/shard_map/ppermute | solution.py:42
  104.3 1.4 fusion.100
  105.7 2.1 copy.73
  107.8 18.2 %collective-permute-start.2 = (f32[14,8,22,3]{2,1,3,0:T(8,128)S(1)}, f32[14,8,22,3]{2,1,3,0:T(8,128)S(1)}, u32[]{:S(2)}, u32[]{:S(2)}) collective-permute-start(f32[14,8,22,3]{2,1,3,0:T(8,128)S(1)} %copy.73), channel_id=1, source_target_pairs={{0,8},{8,16},{16,24},{24,32},{32,40},{40,48},{48,56},{56,0},{1,9},... | collective-permute-start | bytes 88712 | tf_op jit(solution)/shard_map/ppermute | solution.py:40
  126.8 1.6 collective-permute-done.2
  128.3 1.9 copy.75
  130.2 1.4 collective-permute-done.3
  131.6 1.9 copy.76
  133.5 3.0 %pad_maximum_fusion = f32[14,8,22,134]{3,1,2,0:T(8,128)S(1)} fusion(f32[14,8,22,3]{3,1,2,0:T(8,128)} %copy.76, f32[14,8,3,128]{3,1,2,0:T(8,128)} %copy-done.5, f32[1,8,16,128]{3,1,2,0:T(8,128)S(1)} %bitcast.57, f32[1,8,16,128]{3,1,2,0:T(8,128)S(1)} %bitcast.60, f32[12,8,16,128]{3,1,2,0:T(8,128)} %copy-done.1, f32[14,8,3,128]{3,1,2,0:T(8,128)S(1)} %collective-permute-done, ...), kind=kLoop, calls=%fused_computation.38 | loop fusion | flops 1981056 | bytes 2641408 | tf_op jit(solution)/shard_map/concatenate | solution.py:38
  136.5 1.5 fusion.99
  139.0 1.2 copy.77
  140.2 1.9 collective-permute-start.4
  142.7 5.0 %rev.8 = f32[14,3,22,134]{3,1,2,0:T(4,128)} reverse(f32[14,3,22,134]{3,1,2,0:T(4,128)} %copy-done.2), dimensions={1} | reverse | bytes 990528 | tf_op jit(solution)/shard_map/jit(_flip)/rev | solution.py:109
  147.8 2.5 %copy.79 = f32[14,3,22,134]{3,2,1,0:T(8,128)} copy(f32[14,3,22,134]{3,1,2,0:T(4,128)} %get-tuple-element.23) | data formatting | bytes 990528 | tf_op jit(solution)/shard_map/slice | solution.py:108
  150.3 5.0 %rev.7 = f32[14,3,22,134]{3,1,2,0:T(4,128)} reverse(f32[14,3,22,134]{3,1,2,0:T(4,128)} %get-tuple-element.23), dimensions={1} | reverse | bytes 990528 | tf_op jit(solution)/shard_map/jit(_flip)/rev | solution.py:108
  155.3 10.0 %collective-permute-start.5 = (f32[14,3,22,134]{3,2,1,0:T(8,128)}, f32[14,3,22,134]{3,2,1,0:T(8,128)S(1)}, u32[]{:S(2)}, u32[]{:S(2)}) collective-permute-start(f32[14,3,22,134]{3,2,1,0:T(8,128)} %copy.79), channel_id=1, source_target_pairs={{1,0},{2,1},{3,2},{4,3},{5,4},{6,5},{7,6},{0,7},{9,8},{10,9},{11,1... | collective-permute-start | bytes 1485800 | tf_op jit(solution)/shard_map/ppermute | solution.py:42
  165.2 8.3 %collective-permute-done.4 = f32[14,3,22,134]{3,2,1,0:T(8,128)} collective-permute-done((f32[14,3,22,134]{3,2,1,0:T(8,128)}, f32[14,3,22,134]{3,2,1,0:T(8,128)}, u32[]{:S(2)}, u32[]{:S(2)}) %collective-permute-start.4) | collective-permute-done | bytes 495296 | tf_op jit(solution)/shard_map/ppermute | solution.py:40
  173.5 2.2 %copy_select_fusion.1 = f32[14,3,22,134]{3,1,2,0:T(4,128)S(1)} fusion(f32[14,3,22,134]{3,1,2,0:T(4,128)} %rev.7, f32[14,3,22,134]{3,2,1,0:T(8,128)} %collective-permute-done.4, pred[]{:T(512)S(6)} %eq.36), kind=kLoop, calls=%fused_computation.41 | loop fusion | flops 123816 | bytes 1485793 | tf_op jit(solution)/shard_map/jit(_where)/select_n | solution.py:110
  176.8 19.2 %collective-permute-done.5 = f32[14,3,22,134]{3,2,1,0:T(8,128)S(1)} collective-permute-done((f32[14,3,22,134]{3,2,1,0:T(8,128)}, f32[14,3,22,134]{3,2,1,0:T(8,128)S(1)}, u32[]{:S(2)}, u32[]{:S(2)}) %collective-permute-start.5) | collective-permute-done | bytes 495296 | tf_op jit(solution)/shard_map/ppermute | solution.py:42
  197.7 6.5 %multiply_reduce_fusion = (f32[12,20,132]{2,1,0:T(8,128)S(1)}, f32[12,12,20,132]{3,2,1,0:T(8,128)S(1)}) fusion(f32[12,20,132]{2,1,0:T(8,128)S(1)} %fusion.48, f32[12,20,132]{2,1,0:T(8,128)S(1)} %slice.287, f32[14,14,22,134]{3,2,1,0:T(8,128)S(1)} %copy_dynamic-update-slice_fusion.1), kind=kLoop, calls=%fused_computation.22 | loop fusion | flops 10612800 | bytes 12545280 | tf_op jit(solution)/shard_map/reduce_sum | solution.py:87
  205.2 5.6 %multiply_reduce_fusion.1 = (f32[10,18,130]{2,1,0:T(8,128)S(1)}, f32[12,10,18,130]{3,2,1,0:T(8,128)S(1)}) fusion(f32[10,18,130]{2,1,0:T(8,128)S(1)} %fusion.53, f32[10,18,130]{2,1,0:T(8,128)S(1)} %slice.299, f32[12,12,20,132]{3,2,1,0:T(8,128)S(1)} %get-tuple-element.19), kind=kLoop, calls=%fused_computation.36 | loop fusion | flops 7839000 | bytes 9266400 | tf_op jit(solution)/shard_map/reduce_sum | solution.py:87
  212.2 2.2 %fusion.25 = f32[12,8,16,128]{3,2,1,0:T(8,128)} fusion(f32[12,10,18,130]{3,2,1,0:T(8,128)S(1)} %get-tuple-element.15, f32[8,16,128]{2,1,0:T(8,128)S(1)} %get-tuple-element.29, f32[8,16,128]{2,1,0:T(8,128)S(1)} %slice.316), kind=kLoop, calls=%fused_computation.50 | loop fusion | flops 5111808 | bytes 6422528 | tf_op jit(solution)/shard_map/add | solution.py:97
  (72 shorter events, 15.9 us)
Async XLA Ops:
  0.6 27.2 %copy-start = (f32[1,1,1,40,4096]{4,3,2,1,0:T(8,128)S(1)}, f32[1,1,1,40,4096]{4,3,2,1,0:T(8,128)}, u32[]{:S(2)}) copy-start(f32[1,1,1,40,4096]{4,3,2,1,0:T(8,128)} %param.8) | copy-start | bytes 1966084
  5.5 21.4 %all-to-all-start = ((s32[8,1,20]{2,1,0:T(1,128)}), s32[8,1,20]{2,1,0:T(1,128)S(1)}, u32[]{:S(2)}, u32[]{:S(2)}) async-start(s32[8,1,20]{2,1,0:T(1,128)} %bitcast.4), calls=%async_computation | async-start | bytes 8192 | tf_op jit(solution)/shard_map/all_to_all | solution.py:26
  46.8 11.0 %copy-start.6 = (f32[8,16,128]{2,1,0:T(8,128)S(1)}, f32[8,16,128]{2,1,0:T(8,128)}, u32[]{:S(2)}) copy-start(f32[8,16,128]{2,1,0:T(8,128)} %param.7) | copy-start | bytes 196612
  46.8 11.1 %copy-start.4 = (f32[12,8,16,128]{3,2,1,0:T(8,128)S(1)}, f32[12,8,16,128]{3,2,1,0:T(8,128)}, u32[]{:S(2)}) copy-start(f32[12,8,16,128]{3,2,1,0:T(8,128)} %param.6) | copy-start | bytes 2359300
  54.3 24.2 %all-to-all-start.1 = ((f32[8,8,16,128]{3,1,2,0:T(8,128)}), f32[8,8,16,128]{3,1,2,0:T(8,128)S(1)}, u32[]{:S(2)}, u32[]{:S(2)}) async-start(f32[8,8,16,128]{3,1,2,0:T(8,128)} %fusion.19), calls=%async_computation.1 | async-start | bytes 1048576 | tf_op jit(solution)/shard_map/all_to_all | solution.py:146
  58.1 47.6 %copy-start.1 = (f32[12,8,16,128]{3,1,2,0:T(8,128)}, f32[12,8,16,128]{3,1,2,0:T(8,128)S(1)}, u32[]{:S(2)}) copy-start(f32[12,8,16,128]{3,1,2,0:T(8,128)S(1)} %copy.72) | copy-start | bytes 2359300
  78.6 10.2 %collective-permute-start = (f32[14,8,3,128]{3,1,2,0:T(8,128)S(1)}, f32[14,8,3,128]{3,1,2,0:T(8,128)S(1)}, u32[]{:S(2)}, u32[]{:S(2)}) collective-permute-start(f32[14,8,3,128]{3,1,2,0:T(8,128)S(1)} %get-tuple-element.26), channel_id=1, source_target_pairs={{0,64},{64,128},{128,192},{192,256},{256,320},{320,384},{384,448},... | collective-permute-start | bytes 516104 | tf_op jit(solution)/shard_map/ppermute | solution.py:40
  86.4 17.1 %collective-permute-start.1 = (f32[14,8,3,128]{3,1,2,0:T(8,128)S(1)}, f32[14,8,3,128]{3,1,2,0:T(8,128)S(1)}, u32[]{:S(2)}, u32[]{:S(2)}) collective-permute-start(f32[14,8,3,128]{3,1,2,0:T(8,128)S(1)} %get-tuple-element.27), channel_id=1, source_target_pairs={{64,0},{128,64},{192,128},{256,192},{320,256},{384,320},{448,384},... | collective-permute-start | bytes 516104 | tf_op jit(solution)/shard_map/ppermute | solution.py:42
  103.5 0.7 copy-start.5
  107.8 20.5 %collective-permute-start.2 = (f32[14,8,22,3]{2,1,3,0:T(8,128)S(1)}, f32[14,8,22,3]{2,1,3,0:T(8,128)S(1)}, u32[]{:S(2)}, u32[]{:S(2)}) collective-permute-start(f32[14,8,22,3]{2,1,3,0:T(8,128)S(1)} %copy.73), channel_id=1, source_target_pairs={{0,8},{8,16},{16,24},{24,32},{32,40},{40,48},{48,56},{56,0},{1,9},... | collective-permute-start | bytes 88712 | tf_op jit(solution)/shard_map/ppermute | solution.py:40
  126.7 4.8 %collective-permute-start.3 = (f32[14,8,22,3]{2,1,3,0:T(8,128)S(1)}, f32[14,8,22,3]{2,1,3,0:T(8,128)S(1)}, u32[]{:S(2)}, u32[]{:S(2)}) collective-permute-start(f32[14,8,22,3]{2,1,3,0:T(8,128)S(1)} %copy.74), channel_id=1, source_target_pairs={{8,0},{16,8},{24,16},{32,24},{40,32},{48,40},{56,48},{0,56},{9,1},... | collective-permute-start | bytes 88712 | tf_op jit(solution)/shard_map/ppermute | solution.py:42
  137.9 1.1 copy-start.2
  140.2 33.3 %collective-permute-start.4 = (f32[14,3,22,134]{3,2,1,0:T(8,128)}, f32[14,3,22,134]{3,2,1,0:T(8,128)}, u32[]{:S(2)}, u32[]{:S(2)}) collective-permute-start(f32[14,3,22,134]{3,2,1,0:T(8,128)} %copy.77), channel_id=1, source_target_pairs={{0,1},{1,2},{2,3},{3,4},{4,5},{5,6},{6,7},{7,0},{8,9},{9,10},{10,1... | collective-permute-start | bytes 1485800 | tf_op jit(solution)/shard_map/ppermute | solution.py:40
  155.3 40.7 %collective-permute-start.5 = (f32[14,3,22,134]{3,2,1,0:T(8,128)}, f32[14,3,22,134]{3,2,1,0:T(8,128)S(1)}, u32[]{:S(2)}, u32[]{:S(2)}) collective-permute-start(f32[14,3,22,134]{3,2,1,0:T(8,128)} %copy.79), channel_id=1, source_target_pairs={{1,0},{2,1},{3,2},{4,3},{5,4},{6,5},{7,6},{0,7},{9,8},{10,9},{11,1... | collective-permute-start | bytes 1485800 | tf_op jit(solution)/shard_map/ppermute | solution.py:42
  176.0 20.0 %copy-start.3 = (f32[14,3,22,134]{3,1,2,0:T(4,128)S(1)}, f32[14,3,22,134]{3,1,2,0:T(4,128)}, u32[]{:S(2)}) copy-start(f32[14,3,22,134]{3,1,2,0:T(4,128)} %rev.8) | copy-start | bytes 1485796
where the time goes:
time: 215 us; the launch traced here: 214 us
  waiting for transfers between devices  74.9 us (35%)
  starting transfers between devices  55.8 us (26%)
  local copies, waits for them, and re-layouts  36 us (17%)
  other arithmetic  27.3 us (13%)
  matrix products  19.5 us (9%)
    ppermute x3, waiting for transfers between devices, with_halo(): lax.ppermute(head, axis, [((i + 1) % count, i) for i in range(count)])  35.3 us
    ppermute x3, starting transfers between devices, with_halo(): lax.ppermute(tail, axis, [(i, (i + 1) % count) for i in range(count)])  28 us
    all_to_all x1, waiting for transfers between devices, body(): lax.all_to_all(regions, 'gz', split_axis=0, concat_axis=0, tiled=True)  20.4 us
    reduce_sum x3, other arithmetic, advance(): squares = jnp.sum(orders * orders, axis=0)  12.5 us
    all_to_all x1, starting transfers between devices, side_by_side(): lax.all_to_all(both, axis, split_axis=split_dim, concat_axis=concat_dim,...  12.2 us
    ppermute x3, starting transfers between devices, with_halo(): lax.ppermute(head, axis, [((i + 1) % count, i) for i in range(count)])  12.1 us
    ppermute x3, waiting for transfers between devices, with_halo(): lax.ppermute(tail, axis, [(i, (i + 1) % count) for i in range(count)])  10 us
    all_to_all x1, waiting for transfers between devices, side_by_side(): lax.all_to_all(both, axis, split_axis=split_dim, concat_axis=concat_dim,...  9.17 us
  transfers between devices with their start and end apart: 8, of which 8 were waited for; matrix products, arithmetic and copies ran while one was open for 9% of the time, Pallas kernels for 0%

commit v1 on v0

v1 whole, which is shorter than its diff:
```python
import jax
import jax.numpy as jnp
from jax import lax
from jax.experimental import pallas as pl
from jax.experimental.pallas import tpu as pltpu
from jax.sharding import PartitionSpec as P

F32 = jnp.float32
BF16 = jnp.bfloat16
MESH = pl.DeviceIdType.MESH
NF = 14
SOL = 12
HEAT = 13
KEY, HZ, HX, HY, LIVE, TILE = range(6)
AX = 9
NODES = 48
LOW, HIGH = 14, 15


def iota(shape, axis):
    return lax.broadcasted_iota(jnp.int32, shape, axis)


def split(x):
    high = x.astype(BF16)
    return high, (x - high.astype(F32)).astype(BF16)


def nt(a, b):
    return lax.dot_general(a, b, (((1,), (1,)), ((), ())), preferred_element_type=F32)


def main_neighbours(below, row, above, low, high, r):
    lane = iota(row.shape, 1)
    left = jnp.where(lane == 0, pltpu.roll(low, (128 - (r * 8 + 3)) % 128, 1), pltpu.roll(row, 1, 1))
    right = jnp.where(lane == 127, pltpu.roll(high, (127 - (r * 8 + 4)) % 128, 1), pltpu.roll(row, 127, 1))
    return (below + above) + (pltpu.roll(row, 1, 0) + pltpu.roll(row, 23, 0)) + (left + right)


def strip_neighbours(v):
    return (
        (pltpu.roll(v, 8, 1) + pltpu.roll(v, 120, 1))
        + (pltpu.roll(v, 1, 1) + pltpu.roll(v, 127, 1))
        + (pltpu.roll(v, 1, 0) + pltpu.roll(v, 23, 0))
    )


def grown(c, around, s, drive):
    cc = c * c
    w = c - cc
    rate = w * ((4.0 * c - 2.0) + w * drive) + c * (cc - s)
    return 0.04 * c + 0.16 * around + 0.1 * rate


def kernel(
    tiles,
    grains, solute, thermal, slots, owners, offsets,
    grains_out, solute_out, heat_out,
    ext, alt, bend, squares, drives,
    xp, xr, dp, dr, pk, yr,
    req, rq, lb, prm, xs, gr, gx,
    s_rq, r_rq, s_gx, r_gx, s_z, r_z, s_x, r_x, s_zt, r_zt, s_xt, r_xt, s_d, r_d, s_y, r_y,
):
    me = lax.axis_index("gz")
    ix, iy = lax.axis_index("gx"), lax.axis_index("gy")
    nx, ny = lax.axis_size("gx"), lax.axis_size("gy")
    xside = ({"gx": lax.rem(ix + nx - 1, nx)}, {"gx": lax.rem(ix + 1, nx)})
    yside = ({"gy": lax.rem(iy + ny - 1, ny)}, {"gy": lax.rem(iy + 1, ny)})
    others = [{"gz": lax.rem(me + k, tiles)} for k in range(1, tiles)]
    has_low, has_high = me > 0, me < tiles - 1
    zside = ({"gz": jnp.maximum(me - 1, 0)}, {"gz": jnp.minimum(me + 1, tiles - 1)})
    has = (has_low, has_high)

    barrier = pltpu.get_barrier_semaphore()
    partners = [*xside, *yside, *others]
    for d in partners:
        pl.semaphore_signal(barrier, inc=1, device_id=d, device_id_type=MESH)

    def remote(src, dst, ss, rs, d):
        return pltpu.make_async_remote_copy(
            src_ref=src, dst_ref=dst, send_sem=ss, recv_sem=rs, device_id=d, device_id_type=MESH
        )

    live = owners[...] >= 0
    livef = live.astype(F32)
    off = offsets[...]
    half = (off + (off & 1)) >> 1
    req[...] = jnp.zeros((8, 128), F32)
    req[KEY : KEY + 1, 0:20] = jnp.where(live, owners[...] * 64 + slots[...], -1).astype(F32)
    req[HZ : HZ + 3, 0:20] = half.astype(F32) * livef
    req[LIVE : LIVE + 1, 0:20] = livef
    req[TILE : TILE + 1, 0:20] = livef * me.astype(F32)

    for s, first in ((0, 0), (1, 13)):
        def pack(f, _, s=s, first=first):
            for i in range(3):
                xp[s, f, i * 8 : i * 8 + 8, :] = grains[f, :, first + i, :]
            return 0
        lax.fori_loop(0, 12, pack, 0)
        for i in range(3):
            xp[s, SOL, i * 8 : i * 8 + 8, :] = solute[:, first + i, :]

    pl.semaphore_wait(barrier, len(partners))

    request = [
        remote(req, rq.at[me], s_rq.at[k], r_rq.at[me], d) for k, d in enumerate(others)
    ]
    for c in request:
        c.start()
    xcopy = [
        remote(xp.at[0, 0:13], xr.at[1, 0:13], s_x.at[0], r_x.at[1], xside[0]),
        remote(xp.at[1, 0:13], xr.at[0, 0:13], s_x.at[1], r_x.at[0], xside[1]),
    ]
    for c in xcopy:
        c.start()
    zrows = ((0, 11), (5, 0))
    zcopy = []
    for d in range(2):
        a, b = zrows[d]
        zcopy.append((
            remote(grains.at[:, a : a + 3], ext.at[0:12, b : b + 3, 0:16], s_z.at[d], r_z.at[d], zside[d]),
            remote(solute.at[a : a + 3], ext.at[SOL, b : b + 3, 0:16], s_z.at[2 + d], r_z.at[2 + d], zside[d]),
        ))

        @pl.when(has[d])
        def _(d=d):
            for c in zcopy[d]:
                c.start()

    def place(f, _):
        for z in range(8):
            ext[f, 3 + z, 0:16, :] = grains[f, z]
        return 0
    lax.fori_loop(0, 12, place, 0)
    for z in range(8):
        ext[SOL, 3 + z, 0:16, :] = solute[z]

    row8, lane8 = iota((8, 128), 0), iota((8, 128), 1) >> 4
    def turn(g, _):
        rows = pl.ds(pl.multiple_of(g * 8, 8), 8)
        for c in range(32):
            v = thermal[rows, c * 128 : c * 128 + 128]
            for k in (1, 2, 4):
                rb, lbit = (row8 & k) != 0, (lane8 & k) != 0
                a = pltpu.roll(pltpu.roll(v, 8 - k, 0), 16 * k, 1)
                b = pltpu.roll(pltpu.roll(v, k, 0), 128 - 16 * k, 1)
                v = jnp.where(rb == lbit, v, jnp.where(lbit, a, b))
            lb[g, c // 2, (c % 2) * 8 : (c % 2) * 8 + 8, :] = v
        return 0
    lax.fori_loop(0, 5, turn, 0)
    rq[me] = req[...]
    xs[...] = jnp.zeros(xs.shape, F32)

    for k in range(1, tiles):
        src = lax.rem(me + tiles - k, tiles)
        remote(req, rq.at[src], s_rq.at[k - 1], r_rq.at[src], others[k - 1]).wait_recv()

    lists = [jnp.zeros((8, 128), F32), jnp.zeros((8, 128), F32)]
    for t in range(tiles):
        v = rq[t]
        lists[t // 4] = lists[t // 4] + (pltpu.roll(v, 32 * (t % 4), 1) if t % 4 else v)
    for h in range(2):
        prm[5 + h] = lists[h]
    base = me * 64
    for g in range(5):
        slot_of = base + g * 8 + (iota((128, 128), 0) >> 4)
        total = jnp.zeros((8, 128), F32)
        for h in range(2):
            match = jnp.where(lists[h][KEY : KEY + 1, :] == slot_of.astype(F32), 1.0, 0.0).astype(BF16)
            total = total + nt(lists[h].astype(BF16), match)
        prm[g] = total

    def choose(g, _):
        v = prm[g]
        hz, hx = v[HZ : HZ + 1, :], v[HX : HX + 1, :]
        layers = [jnp.zeros((16, 128), F32) for _ in range(5)]
        for p in range(16):
            part = lb[g, p]
            for a in range(5):
                layers[a] = layers[a] + jnp.where(hz == float(a - p), part, 0.0)
        at = iota((16, 128), 0).astype(F32) + hx
        lanes = pl.ds(pl.multiple_of(g * 128, 128), 128)
        for a in range(5):
            for b in range(AX):
                xs[a * AX + b : a * AX + b + 1, lanes] = jnp.sum(
                    jnp.where(at == float(b), layers[a], 0.0), axis=0, keepdims=True
                )
        return 0
    lax.fori_loop(0, 5, choose, 0)

    hi, lo = split(xs[...])
    both = jnp.concatenate([hi, lo], axis=0)
    where_to = []
    for g in range(5):
        v = prm[g]
        spot = v[HY : HY + 1, :] + 128.0 * v[TILE : TILE + 1, :] + (iota((1, 128), 1) & 15).astype(F32)
        where_to.append(jnp.where(v[LIVE : LIVE + 1, :] > 0.5, spot, -4096.0))
    where_to = jnp.concatenate(where_to, axis=1)
    answer = []
    for k in range(tiles - 1, -1, -1):
        t = lax.rem(me + k, tiles)
        line = (iota((128, 640), 0) + t * 128).astype(F32)
        onto = jnp.where(line == where_to, 1.0, 0.0).astype(BF16)
        out = nt(both, onto)
        gr[t] = out[0:NODES] + out[NODES : 2 * NODES]
        if k:
            c = remote(gr.at[t], gx.at[me], s_gx.at[k - 1], r_gx.at[me], others[k - 1])
            c.start()
            answer.append(c)

    def unpack_x(f):
        for z in range(8):
            ext[f, 3 + z, 16:19, :] = xr[1, f, pl.ds(z, 3, stride=8), :]
            ext[f, 3 + z, 21:24, :] = xr[0, f, pl.ds(z, 3, stride=8), :]

    parity = jnp.max(jnp.where(live, off & 1, 0).astype(F32), axis=1, keepdims=True)
    bz, bx, by = parity[0:1], parity[1:2], parity[2:3]
    node, cell = iota((128, 128), 0), iota((128, 128), 1).astype(F32)
    wy = jnp.maximum(0.0, 1.0 - jnp.abs(cell - (2.0 * node.astype(F32) - by)) * 0.5)
    wy = jnp.where(node <= 64, wy, 0.0).astype(BF16)
    ci, ki = iota((128, NODES), 0), iota((128, NODES), 1)
    az = (ki * 57) >> 9
    ax = ki - AX * az
    wz = jnp.maximum(0.0, 1.0 - jnp.abs((ci >> 4).astype(F32) - (2.0 * az.astype(F32) - bz)) * 0.5)
    wx = jnp.maximum(0.0, 1.0 - jnp.abs((ci & 15).astype(F32) - (2.0 * ax.astype(F32) - bx)) * 0.5)
    wzx = (wz * wx).astype(BF16)

    grid = gr[me]
    for k in range(1, tiles):
        src = lax.rem(me + tiles - k, tiles)
        remote(gr.at[src], gx.at[src], s_gx.at[k - 1], r_gx.at[src], others[k - 1]).wait_recv()
        grid = grid + gx[src]
    hi, lo = split(grid)
    fine = jnp.dot(jnp.concatenate([hi, lo], axis=0), wy, preferred_element_type=F32)
    fine = fine[0:NODES] + fine[NODES : 2 * NODES]
    hi, lo = split(fine)
    heat = jnp.dot(wzx, hi, preferred_element_type=F32) + jnp.dot(wzx, lo, preferred_element_type=F32)
    heat = heat.reshape(8, 16, 128)
    heat_out[...] = heat
    for z in range(8):
        ext[HEAT, 3 + z, 0:16, :] = heat[z]
    for s, first in ((0, 0), (1, 13)):
        for i in range(3):
            xp[s, HEAT, i * 8 : i * 8 + 8, :] = heat[:, first + i, :]
    xheat = [
        remote(xp.at[0, HEAT], xr.at[1, HEAT], s_xt.at[0], r_xt.at[1], xside[0]),
        remote(xp.at[1, HEAT], xr.at[0, HEAT], s_xt.at[1], r_xt.at[0], xside[1]),
    ]
    for c in xheat:
        c.start()
    zheat = []
    for d in range(2):
        a, b = zrows[d]
        zheat.append(remote(
            ext.at[HEAT, 3 + a : 6 + a, 0:16], ext.at[HEAT, b : b + 3, 0:16], s_zt.at[d], r_zt.at[d], zside[d]
        ))

        @pl.when(has[d])
        def _(d=d):
            zheat[d].start()

    for c in xcopy:
        c.wait_recv()
    for c in xheat:
        c.wait_recv()

    order = ((2, 1), (0, 1))
    shown = ((0, 1), (7, 6))
    dcopy = []
    for d in range(2):
        for s in range(2):
            near, far = order[s]
            z1, z2 = shown[d]
            for k, (i, z) in enumerate(((near, z1), (near, z2), (far, z1))):
                for f in range(NF):
                    dp[2 * d + s, k, f : f + 1, :] = xr[s, f, i * 8 + z : i * 8 + z + 1, :]
            dcopy.append(remote(
                dp.at[2 * d + s], dr.at[2 * d + s], s_d.at[2 * d + s], r_d.at[2 * d + s], zside[d]
            ))

        @pl.when(has[d])
        def _(d=d):
            for s in range(2):
                dcopy[2 * d + s].start()

    def unpack_all(f, _):
        unpack_x(f)
        return 0
    lax.fori_loop(0, NF, unpack_all, 0)

    for d in range(2):
        @pl.when(has[1 - d])
        def _(d=d):
            for c in zcopy[d]:
                c.wait_recv()
            zheat[d].wait_recv()
            for s in range(2):
                dcopy[2 * d + s].wait_recv()
            e1, e2 = ((11, 12), (2, 1))[d]
            for s in range(2):
                x1, x2 = ((23, 22), (16, 17))[s]
                for k, (e, x) in enumerate(((e1, x1), (e2, x1), (e1, x2))):
                    for f in range(NF):
                        ext[f, e, x : x + 1, :] = dr[2 * d + s, k, f : f + 1, :]

        @pl.when(jnp.logical_not(has[1 - d]))
        def _(d=d):
            def mirror(f, _):
                for i in range(3):
                    if d:
                        ext[f, 2 - i] = ext[f, 3 + i]
                    else:
                        ext[f, 11 + i] = ext[f, 10 - i]
                return 0
            lax.fori_loop(0, NF, mirror, 0)

    slot = iota((24, 128), 1) >> 3
    def pack_y(f, _):
        v = jnp.zeros((24, 128), F32)
        for r in range(14):
            v = jnp.where(slot == r, pltpu.roll(ext[f, r], r * 8 + 4, 1), v)
        pk[f] = v
        return 0
    lax.fori_loop(0, NF, pack_y, 0)
    ycopy = [
        remote(pk, yr.at[1], s_y.at[0], r_y.at[1], yside[0]),
        remote(pk, yr.at[0], s_y.at[1], r_y.at[0], yside[1]),
    ]
    for c in ycopy:
        c.start()
    for c in ycopy:
        c.wait_recv()
    upper = (iota((24, 128), 1) & 7) >= 4
    def unpack_y(f, _):
        own = pk[f]
        ext[f, LOW] = jnp.where(upper, own, yr[0, f])
        ext[f, HIGH] = jnp.where(upper, yr[1, f], own)
        return 0
    lax.fori_loop(0, NF, unpack_y, 0)

    def step(src, dst, first, last):
        def sums(r, _):
            s = src[0, r] * src[0, r]
            for f in range(1, 12):
                s = s + src[f, r] * src[f, r]
            u = src[SOL, r]
            squares[r] = s
            bend[r] = u - 0.5 * s
            drives[r] = 60.0 * (1.0 - ext[HEAT, r] - 0.5 * u)
            return 0
        lax.fori_loop(0, 16, sums, 0)
        final = dst is None

        def fields(f, _):
            low, high = src[f, LOW], src[f, HIGH]
            for r in range(first, last):
                c = src[f, r]
                around = main_neighbours(src[f, r - 1], c, src[f, r + 1], low, high, r)
                v = grown(c, around, squares[r], drives[r])
                if final:
                    grains_out[f, r - 3] = v[0:16]
                else:
                    dst[f, r] = v
            if not final:
                for r, c in ((LOW, low), (HIGH, high)):
                    dst[f, r] = grown(c, strip_neighbours(c), squares[r], drives[r])
            return 0
        lax.fori_loop(0, 12, fields, 0)
        low, high = bend[LOW], bend[HIGH]
        for r in range(first, last):
            c = bend[r]
            lap = main_neighbours(bend[r - 1], c, bend[r + 1], low, high, r) - 6.0 * c
            v = src[SOL, r] + 0.15 * lap
            if final:
                solute_out[r - 3] = v[0:16]
            else:
                dst[SOL, r] = v
        if not final:
            for r, c in ((LOW, low), (HIGH, high)):
                dst[SOL, r] = src[SOL, r] + 0.15 * (strip_neighbours(c) - 6.0 * c)

    step(ext, alt, 1, 13)
    step(alt, ext, 2, 12)
    step(ext, None, 3, 11)

    for c in [*request, *xcopy, *answer, *xheat, *ycopy]:
        c.wait_send()
    for d in range(2):
        @pl.when(has[d])
        def _(d=d):
            for c in (*zcopy[d], zheat[d], dcopy[2 * d], dcopy[2 * d + 1]):
                c.wait_send()


def body(grains, solute, thermal, block_slot, block_owner, block_offset):
    tiles = lax.axis_size("gz")
    vmem = pl.BlockSpec(memory_space=pltpu.VMEM)
    dma = pltpu.SemaphoreType.DMA
    import functools

    return pl.pallas_call(
        functools.partial(kernel, tiles),
        out_shape=(
            jax.ShapeDtypeStruct(grains.shape, F32),
            jax.ShapeDtypeStruct(solute.shape, F32),
            jax.ShapeDtypeStruct(solute.shape, F32),
        ),
        in_specs=[vmem] * 6,
        out_specs=(vmem,) * 3,
        scratch_shapes=[
            pltpu.VMEM((NF, 16, 24, 128), F32),
            pltpu.VMEM((13, 16, 24, 128), F32),
            pltpu.VMEM((16, 24, 128), F32),
            pltpu.VMEM((16, 24, 128), F32),
            pltpu.VMEM((16, 24, 128), F32),
            pltpu.VMEM((2, NF, 24, 128), F32),
            pltpu.VMEM((2, NF, 24, 128), F32),
            pltpu.VMEM((4, 3, 16, 128), F32),
            pltpu.VMEM((4, 3, 16, 128), F32),
            pltpu.VMEM((NF, 24, 128), F32),
            pltpu.VMEM((2, NF, 24, 128), F32),
            pltpu.VMEM((8, 128), F32),
            pltpu.VMEM((tiles, 8, 128), F32),
            pltpu.VMEM((5, 16, 16, 128), F32),
            pltpu.VMEM((7, 8, 128), F32),
            pltpu.VMEM((NODES, 640), F32),
            pltpu.VMEM((tiles, NODES, 128), F32),
            pltpu.VMEM((tiles, NODES, 128), F32),
            dma((tiles,)), dma((tiles,)), dma((tiles,)), dma((tiles,)),
            dma((4,)), dma((4,)), dma((2,)), dma((2,)),
            dma((2,)), dma((2,)), dma((2,)), dma((2,)),
            dma((4,)), dma((4,)), dma((2,)), dma((2,)),
        ],
        compiler_params=pltpu.CompilerParams(
            collective_id=0, has_side_effects=True, vmem_limit_bytes=48 * 1024 * 1024
        ),
    )(
        grains,
        solute,
        thermal.reshape(thermal.shape[3], thermal.shape[4]),
        block_slot.reshape(1, -1),
        block_owner.reshape(1, -1),
        block_offset.reshape(3, -1),
    )


def solution(mesh):
    in_specs = (
        P(None, "gz", "gx", "gy"),
        P("gz", "gx", "gy"),
        P("gz", "gx", "gy", None, None),
        P("gz", "gx", "gy", None),
        P("gz", "gx", "gy", None),
        P("gz", "gx", "gy", None, None),
    )
    out_specs = (P(None, "gz", "gx", "gy"), P("gz", "gx", "gy"), P("gz", "gx", "gy"))
    return jax.shard_map(body, mesh=mesh, in_specs=in_specs, out_specs=out_specs, check_vma=False)
```

time: 215 us -> 83.2 us (0.39)
  the two profiles are of different devices: /device:TPU:15 before, /device:TPU:1 now
where the time goes in v1:
time: 83.2 us; the launch traced here: 82.9 us
  Pallas kernels  75.7 us (91%)
  local copies, waits for them, and re-layouts  6.54 us (8%)
    pallas_call x1, Pallas kernels, body(): pl.pallas_call(functools.partial(kernel, tiles), out_shape=(jax.ShapeDtyp...  75.7 us
    unnamed x16, local copies, waits for them, and re-layouts  6.54 us

profile of v1, /device:TPU:1, one launch (start us, length us, event | category | flops | bytes accessed | tf_op | source)
XLA Modules:
  0.0 82.9 jit_solution(13919857498005456871)
XLA Ops:
  0.6 0.0 copy-start.5
  0.6 0.7 copy-done.5
  1.3 0.0 copy-start.3
  1.3 0.0 copy-start.4
  1.3 0.7 copy-done.3
  2.0 0.0 copy-done.4
  2.0 0.0 copy-start
  2.0 1.1 %copy-done = f32[12,8,16,128]{3,2,1,0:T(8,128)S(1)} copy-done((f32[12,8,16,128]{3,2,1,0:T(8,128)S(1)}, f32[12,8,16,128]{3,2,1,0:T(8,128)}, u32[]{:S(2)}) %copy-start) | copy-done | bytes 786456
  3.1 0.0 copy-start.1
  3.1 1.1 %copy-done.1 = f32[1,1,1,40,4096]{4,3,2,1,0:T(8,128)S(1)} copy-done((f32[1,1,1,40,4096]{4,3,2,1,0:T(8,128)S(1)}, f32[1,1,1,40,4096]{4,3,2,1,0:T(8,128)}, u32[]{:S(2)}) %copy-start.1) | copy-done | bytes 655384
  4.2 0.0 copy-start.2
  4.2 0.8 %copy-done.2 = f32[8,16,128]{2,1,0:T(8,128)S(1)} copy-done((f32[8,16,128]{2,1,0:T(8,128)S(1)}, f32[8,16,128]{2,1,0:T(8,128)}, u32[]{:S(2)}) %copy-start.2) | copy-done | bytes 65560
  5.0 75.7 %shard_map.85 = (f32[12,8,16,128]{3,2,1,0:T(8,128)S(1)}, f32[8,16,128]{2,1,0:T(8,128)S(1)}, f32[8,16,128]{2,1,0:T(8,128)S(1)}) custom-call(f32[12,8,16,128]{3,2,1,0:T(8,128)S(1)} %copy-done, f32[8,16,128]{2,1,0:T(8,128)S(1)} %copy-done.2, f32[40,4096]{1,0:T(8,128)S(1)} %bitcast.6, s32[1,20]{1,0:T(1,128)S(1)} %bitcast.8, s32[1,20]{1,0:T(1,128)S(1)} %bitcast.9, ...), custom_call_target="tpu_custom_call" | custom-call | tf_op jit(solution)/shard_map/pallas_call | solution.py:401
  80.8 0.9 %copy.15 = f32[12,8,16,128]{3,2,1,0:T(8,128)} copy(f32[12,8,16,128]{3,2,1,0:T(8,128)S(1)} %get-tuple-element.6) | data formatting | bytes 1572864
  81.6 0.6 copy.16
  82.3 0.6 copy.17
  (1 shorter events, 0.0 us)
Async XLA Ops:
  0.6 0.7 copy-start.5
  1.3 0.7 copy-start.3
  1.3 0.7 copy-start.4
  2.0 1.1 %copy-start = (f32[12,8,16,128]{3,2,1,0:T(8,128)S(1)}, f32[12,8,16,128]{3,2,1,0:T(8,128)}, u32[]{:S(2)}) copy-start(f32[12,8,16,128]{3,2,1,0:T(8,128)} %grains.1) | copy-start | bytes 2359300
  3.1 1.1 %copy-start.1 = (f32[1,1,1,40,4096]{4,3,2,1,0:T(8,128)S(1)}, f32[1,1,1,40,4096]{4,3,2,1,0:T(8,128)}, u32[]{:S(2)}) copy-start(f32[1,1,1,40,4096]{4,3,2,1,0:T(8,128)} %param.8) | copy-start | bytes 1966084
  4.2 0.8 %copy-start.2 = (f32[8,16,128]{2,1,0:T(8,128)S(1)}, f32[8,16,128]{2,1,0:T(8,128)}, u32[]{:S(2)}) copy-start(f32[8,16,128]{2,1,0:T(8,128)} %solute.1) | copy-start | bytes 196612

commit v2 on v1

--- a/solution.py
+++ b/solution.py
@@ -11,6 +11,7 @@
 NF = 14
 SOL = 12
 HEAT = 13
+DIRECT = 7
 KEY, HZ, HX, HY, LIVE, TILE = range(6)
 AX = 9
 NODES = 48
@@ -30,11 +31,18 @@
     return lax.dot_general(a, b, (((1,), (1,)), ((), ())), preferred_element_type=F32)
 
 
-def main_neighbours(below, row, above, low, high, r):
-    lane = iota(row.shape, 1)
-    left = jnp.where(lane == 0, pltpu.roll(low, (128 - (r * 8 + 3)) % 128, 1), pltpu.roll(row, 1, 1))
-    right = jnp.where(lane == 127, pltpu.roll(high, (127 - (r * 8 + 4)) % 128, 1), pltpu.roll(row, 127, 1))
-    return (below + above) + (pltpu.roll(row, 1, 0) + pltpu.roll(row, 23, 0)) + (left + right)
+def edges(low, high):
+    return jnp.where((iota(low.shape, 1) & 7) == 3, low, pltpu.roll(high, 126, 1))
+
+
+def main_neighbours(below, row, above, edge, r):
+    n = below.shape[0]
+    lane = iota(below.shape, 1)
+    beyond = pltpu.roll(edge, (125 - r * 8) % 128, 1)
+    inside = row[0:n]
+    left = jnp.where(lane == 0, beyond, pltpu.roll(inside, 1, 1))
+    right = jnp.where(lane == 127, beyond, pltpu.roll(inside, 127, 1))
+    return (below + above) + (pltpu.roll(row, 1, 0)[0:n] + pltpu.roll(row, 23, 0)[0:n]) + (left + right)
 
 
 def strip_neighbours(v):
@@ -57,9 +65,11 @@
     grains, solute, thermal, slots, owners, offsets,
     grains_out, solute_out, heat_out,
     ext, alt, bend, squares, drives,
-    xp, xr, dp, dr, pk, yr,
-    req, rq, lb, prm, xs, gr, gx,
-    s_rq, r_rq, s_gx, r_gx, s_z, r_z, s_x, r_x, s_zt, r_zt, s_xt, r_xt, s_d, r_d, s_y, r_y,
+    xp, xr, relay, dp, dr, pk, yr,
+    hk, hy, hxz, hxy, hyz,
+    stored, lists_in, req, rq, lb, prm, xs, gr, gx,
+    loads, s_rq, r_rq, s_gx, r_gx, s_z, r_z, s_x, r_x, s_zt, r_zt, s_xt, r_xt, s_d, r_d, s_y, r_y,
+    s_relay, r_relay, s_hy, r_hy, s_hxz, r_hxz, s_hxy, r_hxy, s_hyz, r_hyz,
 ):
     me = lax.axis_index("gz")
     ix, iy = lax.axis_index("gx"), lax.axis_index("gy")
@@ -68,78 +78,114 @@
     yside = ({"gy": lax.rem(iy + ny - 1, ny)}, {"gy": lax.rem(iy + 1, ny)})
     others = [{"gz": lax.rem(me + k, tiles)} for k in range(1, tiles)]
     has_low, has_high = me > 0, me < tiles - 1
+    relays = nx == 8
+    ax4 = lax.rem(ix, 4)
+    far = (ax4 == 0, ax4 == 3) if relays else (ix < 0, ix < 0)
+    relaying = (ax4 == 1, ax4 == 2)
+    across = 6 + 2 * lax.rem(ix, 2) - ix
     zside = ({"gz": jnp.maximum(me - 1, 0)}, {"gz": jnp.minimum(me + 1, tiles - 1)})
     has = (has_low, has_high)
 
+    bring = [
+        pltpu.make_async_copy(slots, lists_in.at[0], loads.at[0]),
+        pltpu.make_async_copy(owners, lists_in.at[1], loads.at[1]),
+        pltpu.make_async_copy(offsets, lists_in.at[2:5], loads.at[2]),
+        pltpu.make_async_copy(grains, ext.at[0:12, 3:11, 0:16], loads.at[3]),
+        pltpu.make_async_copy(solute, ext.at[SOL, 3:11, 0:16], loads.at[4]),
+        pltpu.make_async_copy(thermal, stored, loads.at[5]),
+    ]
+    for c in bring:
+        c.start()
+
     barrier = pltpu.get_barrier_semaphore()
-    partners = [*xside, *yside, *others]
+    xy = [[{**xside[s], **yside[t]} for s in range(2)] for t in range(2)]
+    xz = [[{**xside[s], **zside[d]} for s in range(2)] for d in range(2)]
+    yz = [[{**yside[t], **zside[d]} for d in range(2)] for t in range(2)]
+    partners = [*xside, *yside, *others, *xy[0], *xy[1]]
+    if relays:
+        partners.append({"gx": across})
     for d in partners:
         pl.semaphore_signal(barrier, inc=1, device_id=d, device_id_type=MESH)
+    for d in range(2):
+        @pl.when(has[d])
+        def _(d=d):
+            for p in (*xz[d], yz[0][d], yz[1][d]):
+                pl.semaphore_signal(barrier, inc=1, device_id=p, device_id_type=MESH)
 
     def remote(src, dst, ss, rs, d):
         return pltpu.make_async_remote_copy(
             src_ref=src, dst_ref=dst, send_sem=ss, recv_sem=rs, device_id=d, device_id_type=MESH
         )
 
-    live = owners[...] >= 0
+    for c in bring[0:3]:
+        c.wait()
+    live = lists_in[1] >= 0
     livef = live.astype(F32)
-    off = offsets[...]
-    half = (off + (off & 1)) >> 1
+    off = [lists_in[2 + i] for i in range(3)]
     req[...] = jnp.zeros((8, 128), F32)
-    req[KEY : KEY + 1, 0:20] = jnp.where(live, owners[...] * 64 + slots[...], -1).astype(F32)
-    req[HZ : HZ + 3, 0:20] = half.astype(F32) * livef
+    req[KEY : KEY + 1, 0:20] = jnp.where(live, lists_in[1] * 64 + lists_in[0], -1).astype(F32)
+    for i in range(3):
+        req[HZ + i : HZ + i + 1, 0:20] = ((off[i] + (off[i] & 1)) >> 1).astype(F32) * livef
     req[LIVE : LIVE + 1, 0:20] = livef
     req[TILE : TILE + 1, 0:20] = livef * me.astype(F32)
 
+    for c in bring[3:5]:
+        c.wait()
     for s, first in ((0, 0), (1, 13)):
         def pack(f, _, s=s, first=first):
             for i in range(3):
-                xp[s, f, i * 8 : i * 8 + 8, :] = grains[f, :, first + i, :]
+                xp[s, f, i * 8 : i * 8 + 8, :] = ext[f, 3:11, first + i, :]
             return 0
-        lax.fori_loop(0, 12, pack, 0)
-        for i in range(3):
-            xp[s, SOL, i * 8 : i * 8 + 8, :] = solute[:, first + i, :]
-
-    pl.semaphore_wait(barrier, len(partners))
+        lax.fori_loop(0, 13, pack, 0)
+
+    pl.semaphore_wait(barrier, len(partners) + 4 * (jnp.minimum(me, 1) + jnp.minimum(tiles - 1 - me, 1)))
 
     request = [
         remote(req, rq.at[me], s_rq.at[k], r_rq.at[me], d) for k, d in enumerate(others)
     ]
     for c in request:
         c.start()
-    xcopy = [
-        remote(xp.at[0, 0:13], xr.at[1, 0:13], s_x.at[0], r_x.at[1], xside[0]),
-        remote(xp.at[1, 0:13], xr.at[0, 0:13], s_x.at[1], r_x.at[0], xside[1]),
+    xcopy = []
+    for s in range(2):
+        xcopy.append(remote(xp.at[s, 0:DIRECT], xr.at[1 - s, 0:DIRECT], s_x.at[s], r_x.at[1 - s], xside[s]))
+    for s in range(2):
+        xcopy.append(remote(
+            xp.at[s, DIRECT:13], xr.at[1 - s, DIRECT:13], s_x.at[2 + s], r_x.at[3 - s], xside[s]
+        ))
+    by_way = [remote(xp.at[s, DIRECT:13], relay, s_x.at[2 + s], r_relay, xside[1 - s]) for s in range(2)]
+    onward = [
+        remote(relay, xr.at[1 - s, DIRECT:13], s_relay, r_x.at[3 - s], {"gx": across}) for s in range(2)
     ]
-    for c in xcopy:
-        c.start()
+    if relays:
+        for s in range(2):
+            @pl.when(far[s])
+            def _(s=s):
+                by_way[s].start()
+    for s in range(2):
+        xcopy[s].start()
+    for s in range(2):
+        @pl.when(jnp.logical_not(far[s]))
+        def _(s=s):
+            xcopy[2 + s].start()
     zrows = ((0, 11), (5, 0))
     zcopy = []
     for d in range(2):
         a, b = zrows[d]
-        zcopy.append((
-            remote(grains.at[:, a : a + 3], ext.at[0:12, b : b + 3, 0:16], s_z.at[d], r_z.at[d], zside[d]),
-            remote(solute.at[a : a + 3], ext.at[SOL, b : b + 3, 0:16], s_z.at[2 + d], r_z.at[2 + d], zside[d]),
+        zcopy.append(remote(
+            ext.at[0:13, 3 + a : 6 + a, 0:16], ext.at[0:13, b : b + 3, 0:16], s_z.at[d], r_z.at[d], zside[d]
         ))
 
         @pl.when(has[d])
         def _(d=d):
-            for c in zcopy[d]:
-                c.start()
-
-    def place(f, _):
-        for z in range(8):
-            ext[f, 3 + z, 0:16, :] = grains[f, z]
-        return 0
-    lax.fori_loop(0, 12, place, 0)
-    for z in range(8):
-        ext[SOL, 3 + z, 0:16, :] = solute[z]
+            zcopy[d].start()
 
     row8, lane8 = iota((8, 128), 0), iota((8, 128), 1) >> 4
+    bring[5].wait()
+
     def turn(g, _):
         rows = pl.ds(pl.multiple_of(g * 8, 8), 8)
         for c in range(32):
-            v = thermal[rows, c * 128 : c * 128 + 128]
+            v = stored[rows, c * 128 : c * 128 + 128]
             for k in (1, 2, 4):
                 rb, lbit = (row8 & k) != 0, (lane8 & k) != 0
                 a = pltpu.roll(pltpu.roll(v, 8 - k, 0), 16 * k, 1)
@@ -154,6 +200,13 @@
     for k in range(1, tiles):
         src = lax.rem(me + tiles - k, tiles)
         remote(req, rq.at[src], s_rq.at[k - 1], r_rq.at[src], others[k - 1]).wait_recv()
+
+    if relays:
+        for s in range(2):
+            @pl.when(relaying[s])
+            def _(s=s):
+                by_way[s].wait_recv()
+                onward[s].start()
 
     lists = [jnp.zeros((8, 128), F32), jnp.zeros((8, 128), F32)]
     for t in range(tiles):
@@ -208,13 +261,64 @@
             c.start()
             answer.append(c)
 
+    def mirror(fields, rows):
+        for d in range(2):
+            @pl.when(jnp.logical_not(has[1 - d]))
+            def _(d=d):
+                def one(f, _):
+                    for i in range(3):
+                        if d:
+                            ext[f, 2 - i, rows] = ext[f, 3 + i, rows]
+                        else:
+                            ext[f, 11 + i, rows] = ext[f, 10 - i, rows]
+                    return 0
+                lax.fori_loop(*fields, one, 0)
+
+    for d in range(2):
+        @pl.when(has[1 - d])
+        def _(d=d):
+            zcopy[d].wait_recv()
+    inner, outer = slice(0, 16), slice(16, 24)
+    mirror((0, 13), inner)
+
+    def pack_y(rows, count):
+        slot = iota((count, 128), 1) >> 3
+        def one(f, _):
+            v = jnp.zeros((count, 128), F32)
+            for r in range(14):
+                v = jnp.where(slot == r, pltpu.roll(ext[f, r, rows], r * 8 + 4, 1), v)
+            pk[f, rows] = v
+            return 0
+        lax.fori_loop(0, 13, one, 0)
+
+    def y_copies(rows, k):
+        return [
+            remote(pk.at[:, rows], yr.at[1, :, rows], s_y.at[k], r_y.at[k + 1], yside[0]),
+            remote(pk.at[:, rows], yr.at[0, :, rows], s_y.at[k + 1], r_y.at[k], yside[1]),
+        ]
+
+    def unpack_y(rows, count):
+        upper = (iota((count, 128), 1) & 7) >= 4
+        def one(f, _):
+            own = pk[f, rows]
+            ext[f, LOW, rows] = jnp.where(upper, own, yr[0, f, rows])
+            ext[f, HIGH, rows] = jnp.where(upper, yr[1, f, rows], own)
+            return 0
+        lax.fori_loop(0, 13, one, 0)
+
+    pack_y(inner, 16)
+    yinner = y_copies(inner, 0)
+    for c in yinner:
+        c.start()
+
     def unpack_x(f):
         for z in range(8):
             ext[f, 3 + z, 16:19, :] = xr[1, f, pl.ds(z, 3, stride=8), :]
             ext[f, 3 + z, 21:24, :] = xr[0, f, pl.ds(z, 3, stride=8), :]
 
-    parity = jnp.max(jnp.where(live, off & 1, 0).astype(F32), axis=1, keepdims=True)
-    bz, bx, by = parity[0:1], parity[1:2], parity[2:3]
+    bz, bx, by = [
+        jnp.max(jnp.where(live, o & 1, 0).astype(F32), axis=1, keepdims=True) for o in off
+    ]
     node, cell = iota((128, 128), 0), iota((128, 128), 1).astype(F32)
     wy = jnp.maximum(0.0, 1.0 - jnp.abs(cell - (2.0 * node.astype(F32) - by)) * 0.5)
     wy = jnp.where(node <= 64, wy, 0.0).astype(BF16)
@@ -259,9 +363,41 @@
         def _(d=d):
             zheat[d].start()
 
+    for z in range(8):
+        v = pltpu.roll(heat[z], (z + 3) * 8 + 4, 1)
+        strips = v if z == 0 else jnp.where((iota((16, 128), 1) >> 3) == z + 3, v, strips)
+    hk[...] = strips
+    yheat, xyheat, xzheat, yzheat = [], [], [], []
+    for t in range(2):
+        yheat.append(remote(hk, hy.at[1 - t], s_hy.at[t], r_hy.at[1 - t], yside[t]))
+        for s in range(2):
+            n = 2 * (1 - t) + 1 - s
+            xyheat.append(remote(
+                hk.at[8 * s : 8 * s + 8], hxy.at[n], s_hxy.at[2 * t + s], r_hxy.at[n], xy[t][s]
+            ))
+    for c in (*xyheat, *yheat):
+        c.start()
+    for d in range(2):
+        for s in range(2):
+            n = 2 * d + 1 - s
+            xzheat.append(remote(
+                ext.at[HEAT, (3, 10)[d], 8 * s : 8 * s + 8], hxz.at[n], s_hxz.at[2 * d + s], r_hxz.at[n], xz[d][s]
+            ))
+        for t in range(2):
+            n = 2 * d + 1 - t
+            yzheat.append(remote(hk, hyz.at[n], s_hyz.at[2 * d + t], r_hyz.at[n], yz[t][d]))
+
+        @pl.when(has[d])
+        def _(d=d):
+            for k in (2 * d, 2 * d + 1):
+                xzheat[k].start()
+                yzheat[k].start()
+
+    for c in yinner:
+        c.wait_recv()
+    unpack_y(inner, 16)
+
     for c in xcopy:
-        c.wait_recv()
-    for c in xheat:
         c.wait_recv()
 
     order = ((2, 1), (0, 1))
@@ -272,7 +408,7 @@
             near, far = order[s]
             z1, z2 = shown[d]
             for k, (i, z) in enumerate(((near, z1), (near, z2), (far, z1))):
-                for f in range(NF):
+                for f in range(13):
                     dp[2 * d + s, k, f : f + 1, :] = xr[s, f, i * 8 + z : i * 8 + z + 1, :]
             dcopy.append(remote(
                 dp.at[2 * d + s], dr.at[2 * d + s], s_d.at[2 * d + s], r_d.at[2 * d + s], zside[d]
@@ -286,57 +422,63 @@
     def unpack_all(f, _):
         unpack_x(f)
         return 0
-    lax.fori_loop(0, NF, unpack_all, 0)
+    lax.fori_loop(0, 13, unpack_all, 0)
 
     for d in range(2):
         @pl.when(has[1 - d])
         def _(d=d):
-            for c in zcopy[d]:
-                c.wait_recv()
-            zheat[d].wait_recv()
             for s in range(2):
                 dcopy[2 * d + s].wait_recv()
             e1, e2 = ((11, 12), (2, 1))[d]
             for s in range(2):
                 x1, x2 = ((23, 22), (16, 17))[s]
                 for k, (e, x) in enumerate(((e1, x1), (e2, x1), (e1, x2))):
-                    for f in range(NF):
+                    for f in range(13):
                         ext[f, e, x : x + 1, :] = dr[2 * d + s, k, f : f + 1, :]
+    mirror((0, 13), outer)
+
+    pack_y(outer, 8)
+    youter = y_copies(outer, 2)
+    for c in youter:
+        c.start()
+
+    for c in (*xheat, *yheat):
+        c.wait_recv()
+    for c in xyheat:
+        c.wait_recv()
+    unpack_x(HEAT)
+    lane16, slot16, row8 = iota((16, 128), 1), iota((16, 128), 1) >> 3, iota((8, 128), 0)
+    theirs = ((lane16 & 7) < 4, (lane16 & 7) >= 4)
+    for p in range(2):
+        ext[HEAT, LOW + p, inner] = jnp.where(theirs[p], hy[p], strips)
+        ext[HEAT, LOW + p, outer] = jnp.where(row8 < 4, hxy[2 * p + 1], hxy[2 * p])
+    mirror((HEAT, HEAT + 1), slice(0, 24))
+    for d in range(2):
+        new = (11, 2)[d]
+
+        @pl.when(has[1 - d])
+        def _(d=d, new=new):
+            zheat[d].wait_recv()
+            for k in (2 * d, 2 * d + 1):
+                xzheat[k].wait_recv()
+                yzheat[k].wait_recv()
+            ext[HEAT, new, outer] = jnp.where(row8 < 4, hxz[2 * d + 1], hxz[2 * d])
+            for p in range(2):
+                ext[HEAT, LOW + p, inner] = jnp.where(
+                    theirs[p] & (slot16 == new), pltpu.roll(hyz[2 * d + p], 64, 1), ext[HEAT, LOW + p, inner]
+                )
 
         @pl.when(jnp.logical_not(has[1 - d]))
-        def _(d=d):
-            def mirror(f, _):
-                for i in range(3):
-                    if d:
-                        ext[f, 2 - i] = ext[f, 3 + i]
-                    else:
-                        ext[f, 11 + i] = ext[f, 10 - i]
-                return 0
-            lax.fori_loop(0, NF, mirror, 0)
-
-    slot = iota((24, 128), 1) >> 3
-    def pack_y(f, _):
-        v = jnp.zeros((24, 128), F32)
-        for r in range(14):
-            v = jnp.where(slot == r, pltpu.roll(ext[f, r], r * 8 + 4, 1), v)
-        pk[f] = v
-        return 0
-    lax.fori_loop(0, NF, pack_y, 0)
-    ycopy = [
-        remote(pk, yr.at[1], s_y.at[0], r_y.at[1], yside[0]),
-        remote(pk, yr.at[0], s_y.at[1], r_y.at[0], yside[1]),
-    ]
-    for c in ycopy:
-        c.start()
-    for c in ycopy:
+        def _(d=d, new=new):
+            for p in range(2):
+                v = ext[HEAT, LOW + p, inner]
+                ext[HEAT, LOW + p, inner] = jnp.where(
+                    theirs[p] & (slot16 == new), pltpu.roll(v, (8, 120)[d], 1), v
+                )
+
+    for c in youter:
         c.wait_recv()
-    upper = (iota((24, 128), 1) & 7) >= 4
-    def unpack_y(f, _):
-        own = pk[f]
-        ext[f, LOW] = jnp.where(upper, own, yr[0, f])
-        ext[f, HIGH] = jnp.where(upper, yr[1, f], own)
-        return 0
-    lax.fori_loop(0, NF, unpack_y, 0)
+    unpack_y(outer, 8)
 
     def step(src, dst, first, last):
         def sums(r, _):
@@ -350,15 +492,17 @@
             return 0
         lax.fori_loop(0, 16, sums, 0)
         final = dst is None
+        n = 16 if final else 24
 
         def fields(f, _):
             low, high = src[f, LOW], src[f, HIGH]
+            edge = edges(low, high)[0:n]
             for r in range(first, last):
                 c = src[f, r]
-                around = main_neighbours(src[f, r - 1], c, src[f, r + 1], low, high, r)
-                v = grown(c, around, squares[r], drives[r])
+                around = main_neighbours(src[f, r - 1, 0:n], c, src[f, r + 1, 0:n], edge, r)
+                v = grown(c[0:n], around, squares[r, 0:n], drives[r, 0:n])
                 if final:
-                    grains_out[f, r - 3] = v[0:16]
+                    grains_out[f, r - 3] = v
                 else:
                     dst[f, r] = v
             if not final:
@@ -367,12 +511,13 @@
             return 0
         lax.fori_loop(0, 12, fields, 0)
         low, high = bend[LOW], bend[HIGH]
+        edge = edges(low, high)[0:n]
         for r in range(first, last):
             c = bend[r]
-            lap = main_neighbours(bend[r - 1], c, bend[r + 1], low, high, r) - 6.0 * c
-            v = src[SOL, r] + 0.15 * lap
+            lap = main_neighbours(bend[r - 1, 0:n], c, bend[r + 1, 0:n], edge, r) - 6.0 * c[0:n]
+            v = src[SOL, r, 0:n] + 0.15 * lap
             if final:
-                solute_out[r - 3] = v[0:16]
+                solute_out[r - 3] = v
             else:
                 dst[SOL, r] = v
         if not final:
@@ -380,16 +525,27 @@
                 dst[SOL, r] = src[SOL, r] + 0.15 * (strip_neighbours(c) - 6.0 * c)
 
     step(ext, alt, 1, 13)
+    for d in range(2):
+        @pl.when(has[d])
+        def _(d=d):
+            zcopy[d].wait_send()
+
     step(alt, ext, 2, 12)
     step(ext, None, 3, 11)
 
-    for c in [*request, *xcopy, *answer, *xheat, *ycopy]:
+    for c in [*request, *xcopy, *answer, *xheat, *yinner, *youter, *yheat, *xyheat]:
         c.wait_send()
     for d in range(2):
         @pl.when(has[d])
         def _(d=d):
-            for c in (*zcopy[d], zheat[d], dcopy[2 * d], dcopy[2 * d + 1]):
-                c.wait_send()
+            for k in (2 * d, 2 * d + 1):
+                for c in (dcopy[k], xzheat[k], yzheat[k]):
+                    c.wait_send()
+            zheat[d].wait_send()
+    if relays:
+        @pl.when(relaying[0] | relaying[1])
+        def _():
+            onward[0].wait_send()
 
 
 def body(grains, solute, thermal, block_slot, block_owner, block_offset):
@@ -405,7 +561,7 @@
             jax.ShapeDtypeStruct(solute.shape, F32),
             jax.ShapeDtypeStruct(solute.shape, F32),
         ),
-        in_specs=[vmem] * 6,
+        in_specs=[pl.BlockSpec(memory_space=pltpu.HBM)] * 6,
         out_specs=(vmem,) * 3,
         scratch_shapes=[
             pltpu.VMEM((NF, 16, 24, 128), F32),
@@ -415,10 +571,18 @@
             pltpu.VMEM((16, 24, 128), F32),
             pltpu.VMEM((2, NF, 24, 128), F32),
             pltpu.VMEM((2, NF, 24, 128), F32),
+            pltpu.VMEM((13 - DIRECT, 24, 128), F32),
             pltpu.VMEM((4, 3, 16, 128), F32),
             pltpu.VMEM((4, 3, 16, 128), F32),
-            pltpu.VMEM((NF, 24, 128), F32),
-            pltpu.VMEM((2, NF, 24, 128), F32),
+            pltpu.VMEM((13, 24, 128), F32),
+            pltpu.VMEM((2, 13, 24, 128), F32),
+            pltpu.VMEM((16, 128), F32),
+            pltpu.VMEM((2, 16, 128), F32),
+            pltpu.VMEM((4, 8, 128), F32),
+            pltpu.VMEM((4, 8, 128), F32),
+            pltpu.VMEM((4, 16, 128), F32),
+            pltpu.VMEM((40, 4096), F32),
+            pltpu.VMEM((5, 1, 20), jnp.int32),
             pltpu.VMEM((8, 128), F32),
             pltpu.VMEM((tiles, 8, 128), F32),
             pltpu.VMEM((5, 16, 16, 128), F32),
@@ -426,13 +590,15 @@
             pltpu.VMEM((NODES, 640), F32),
             pltpu.VMEM((tiles, NODES, 128), F32),
             pltpu.VMEM((tiles, NODES, 128), F32),
-            dma((tiles,)), dma((tiles,)), dma((tiles,)), dma((tiles,)),
-            dma((4,)), dma((4,)), dma((2,)), dma((2,)),
+            dma((6,)), dma((tiles,)), dma((tiles,)), dma((tiles,)), dma((tiles,)),
+            dma((2,)), dma((2,)), dma((4,)), dma((4,)),
             dma((2,)), dma((2,)), dma((2,)), dma((2,)),
-            dma((4,)), dma((4,)), dma((2,)), dma((2,)),
+            dma((4,)), dma((4,)), dma((4,)), dma((4,)),
+            dma, dma, dma((2,)), dma((2,)), dma((4,)), dma((4,)),
+            dma((4,)), dma((4,)), dma((4,)), dma((4,)),
         ],
         compiler_params=pltpu.CompilerParams(
-            collective_id=0, has_side_effects=True, vmem_limit_bytes=48 * 1024 * 1024
+            collective_id=0, has_side_effects=True, vmem_limit_bytes=66000000
         ),
     )(
         grains,
@@ -440,7 +606,7 @@
         thermal.reshape(thermal.shape[3], thermal.shape[4]),
         block_slot.reshape(1, -1),
         block_owner.reshape(1, -1),
-        block_offset.reshape(3, -1),
+        block_offset.reshape(3, 1, -1),
     )
 
 

time: 83.2 us -> 69 us (0.83)
  the two profiles are of different devices: /device:TPU:1 before, /device:TPU:97 now
where the time goes in v2:
time: 69 us; the launch traced here: 68.8 us
  Pallas kernels  64.6 us (94%)
  local copies, waits for them, and re-layouts  3.59 us (5%)
    pallas_call x1, Pallas kernels, body(): pl.pallas_call(functools.partial(kernel, tiles), out_shape=(jax.ShapeDtyp...  64.6 us
    unnamed x7, local copies, waits for them, and re-layouts  3.59 us

profile of v2, /device:TPU:97, one launch (start us, length us, event | category | flops | bytes accessed | tf_op | source)
XLA Modules:
  0.0 68.8 jit_solution(9261217036472607520)
XLA Ops:
  0.6 64.6 %shard_map.85 = (f32[12,8,16,128]{3,2,1,0:T(8,128)}, f32[8,16,128]{2,1,0:T(8,128)}, f32[8,16,128]{2,1,0:T(8,128)}) custom-call(f32[12,8,16,128]{3,2,1,0:T(8,128)} %grains.1, f32[8,16,128]{2,1,0:T(8,128)} %solute.1, f32[40,4096]{1,0:T(8,128)} %bitcast.4, s32[1,20]{1,0:T(1,128)} %bitcast.6, s32[1,20]{1,0:T(1,128)} %bitcast.7, s32[3,1,20]{2,1,0:T(1,128)} %bitcast.5), custom_call_target="tpu_custom_call" | custom-call | tf_op jit(solution)/shard_map/pallas_call | solution.py:557
  65.2 0.0 copy-start.1
  65.2 2.1 %copy.12 = f32[12,8,16,128]{3,2,1,0:T(8,128)} copy(f32[12,8,16,128]{3,2,1,0:T(8,128)} %get-tuple-element.6) | data formatting | bytes 1572864
  67.3 0.0 copy-done.1
  67.3 0.0 copy-start
  67.3 0.6 copy.13
  68.0 0.2 copy-done
  68.2 0.6 copy.14
Async XLA Ops:
  65.2 2.1 %copy-start.1 = (f32[8,16,128]{2,1,0:T(8,128)S(1)}, f32[8,16,128]{2,1,0:T(8,128)}, u32[]{:S(2)}) copy-start(f32[8,16,128]{2,1,0:T(8,128)} %get-tuple-element.7) | copy-start | bytes 196612
  67.3 0.9 %copy-start = (f32[8,16,128]{2,1,0:T(8,128)S(1)}, f32[8,16,128]{2,1,0:T(8,128)}, u32[]{:S(2)}) copy-start(f32[8,16,128]{2,1,0:T(8,128)} %get-tuple-element.8) | copy-start | bytes 196612

commit v3 on v2

--- a/solution.py
+++ b/solution.py
@@ -11,7 +11,8 @@
 NF = 14
 SOL = 12
 HEAT = 13
-DIRECT = 7
+DIRECT = 4
+EARLY = 7
 KEY, HZ, HX, HY, LIVE, TILE = range(6)
 AX = 9
 NODES = 48
@@ -31,33 +32,44 @@
     return lax.dot_general(a, b, (((1,), (1,)), ((), ())), preferred_element_type=F32)
 
 
+GROUPS = ((8, 16), (16, 24), (0, 8))
+
+
 def edges(low, high):
     return jnp.where((iota(low.shape, 1) & 7) == 3, low, pltpu.roll(high, 126, 1))
 
 
-def main_neighbours(below, row, above, edge, r):
-    n = below.shape[0]
-    lane = iota(below.shape, 1)
+def along_x(ref, r, a):
+    sub = iota((8, 128), 0)
+    if a == 0:
+        before = jnp.where(sub == 0, ref[r, 23:24, :], pltpu.roll(ref[r, 0:8, :], 1, 0))
+        return before + ref[r, 1:9, :]
+    after = ref[r, a + 1 : a + 9, :]
+    if a == 16:
+        after = jnp.where(sub == 7, ref[r, 0:1, :], after)
+    return ref[r, a - 1 : a + 7, :] + after
+
+
+def main_neighbours(ref, r, a, edge):
+    lane = iota((8, 128), 1)
+    c = ref[r, a : a + 8, :]
     beyond = pltpu.roll(edge, (125 - r * 8) % 128, 1)
-    inside = row[0:n]
-    left = jnp.where(lane == 0, beyond, pltpu.roll(inside, 1, 1))
-    right = jnp.where(lane == 127, beyond, pltpu.roll(inside, 127, 1))
-    return (below + above) + (pltpu.roll(row, 1, 0)[0:n] + pltpu.roll(row, 23, 0)[0:n]) + (left + right)
-
-
-def strip_neighbours(v):
-    return (
-        (pltpu.roll(v, 8, 1) + pltpu.roll(v, 120, 1))
-        + (pltpu.roll(v, 1, 1) + pltpu.roll(v, 127, 1))
-        + (pltpu.roll(v, 1, 0) + pltpu.roll(v, 23, 0))
-    )
+    left = jnp.where(lane == 0, beyond, pltpu.roll(c, 1, 1))
+    right = jnp.where(lane == 127, beyond, pltpu.roll(c, 127, 1))
+    return c, (ref[r - 1, a : a + 8, :] + ref[r + 1, a : a + 8, :]) + along_x(ref, r, a) + (left + right)
+
+
+def strip_neighbours(ref, r, a):
+    c = ref[r, a : a + 8, :]
+    z = pltpu.roll(c, 8, 1) + pltpu.roll(c, 120, 1)
+    y = pltpu.roll(c, 1, 1) + pltpu.roll(c, 127, 1)
+    return c, z + y + along_x(ref, r, a)
 
 
 def grown(c, around, s, drive):
     cc = c * c
     w = c - cc
-    rate = w * ((4.0 * c - 2.0) + w * drive) + c * (cc - s)
-    return 0.04 * c + 0.16 * around + 0.1 * rate
+    return w * ((0.4 * c - 0.2) + w * drive) + c * (0.1 * cc - s) + 0.16 * around
 
 
 def kernel(
@@ -90,8 +102,8 @@
         pltpu.make_async_copy(slots, lists_in.at[0], loads.at[0]),
         pltpu.make_async_copy(owners, lists_in.at[1], loads.at[1]),
         pltpu.make_async_copy(offsets, lists_in.at[2:5], loads.at[2]),
-        pltpu.make_async_copy(grains, ext.at[0:12, 3:11, 0:16], loads.at[3]),
-        pltpu.make_async_copy(solute, ext.at[SOL, 3:11, 0:16], loads.at[4]),
+        pltpu.make_async_copy(grains, ext.at[0:12, 3:11, 8:24], loads.at[3]),
+        pltpu.make_async_copy(solute, ext.at[SOL, 3:11, 8:24], loads.at[4]),
         pltpu.make_async_copy(thermal, stored, loads.at[5]),
     ]
     for c in bring:
@@ -134,7 +146,7 @@
     for s, first in ((0, 0), (1, 13)):
         def pack(f, _, s=s, first=first):
             for i in range(3):
-                xp[s, f, i * 8 : i * 8 + 8, :] = ext[f, 3:11, first + i, :]
+                xp[s, f, i * 8 : i * 8 + 8, :] = ext[f, 3:11, 8 + first + i, :]
             return 0
         lax.fori_loop(0, 13, pack, 0)
 
@@ -171,13 +183,17 @@
     zcopy = []
     for d in range(2):
         a, b = zrows[d]
-        zcopy.append(remote(
-            ext.at[0:13, 3 + a : 6 + a, 0:16], ext.at[0:13, b : b + 3, 0:16], s_z.at[d], r_z.at[d], zside[d]
-        ))
-
-        @pl.when(has[d])
-        def _(d=d):
-            zcopy[d].start()
+        zcopy.append([
+            remote(
+                ext.at[f, 3 + a : 6 + a, 8:24], ext.at[f, b : b + 3, 8:24], s_z.at[2 * k + d], r_z.at[2 * k + d], zside[d]
+            )
+            for k, f in enumerate((slice(0, EARLY), slice(EARLY, 13)))
+        ])
+
+        @pl.when(has[d])
+        def _(d=d):
+            zcopy[d][0].start()
+
 
     row8, lane8 = iota((8, 128), 0), iota((8, 128), 1) >> 4
     bring[5].wait()
@@ -249,18 +265,32 @@
         spot = v[HY : HY + 1, :] + 128.0 * v[TILE : TILE + 1, :] + (iota((1, 128), 1) & 15).astype(F32)
         where_to.append(jnp.where(v[LIVE : LIVE + 1, :] > 0.5, spot, -4096.0))
     where_to = jnp.concatenate(where_to, axis=1)
+    tile_of = lax.rem(me + iota((8, 640), 0), tiles) * 128 + 64
+    last = jnp.where(tile_of.astype(F32) == where_to, 1.0, 0.0).astype(BF16)
+    blank = jnp.zeros((64, 640), BF16)
+    tail = nt(last, jnp.concatenate([blank, hi, blank[0:16]], axis=0))
+    tail = tail + nt(last, jnp.concatenate([blank, lo, blank[0:16]], axis=0))
+    lane, at_last = iota((24, 128), 1), iota((24, 128), 0) == 23
     answer = []
     for k in range(tiles - 1, -1, -1):
         t = lax.rem(me + k, tiles)
         line = (iota((128, 640), 0) + t * 128).astype(F32)
         onto = jnp.where(line == where_to, 1.0, 0.0).astype(BF16)
         out = nt(both, onto)
-        gr[t] = out[0:NODES] + out[NODES : 2 * NODES]
+        out = out[0:NODES] + out[NODES : 2 * NODES]
+        upper = jnp.where(at_last, tail[k : k + 1, :], pltpu.roll(out[24:48], 64, 1))
+        gr[t] = jnp.where(lane < 64, out[0:24], upper)
         if k:
             c = remote(gr.at[t], gx.at[me], s_gx.at[k - 1], r_gx.at[me], others[k - 1])
             c.start()
             answer.append(c)
 
+    for d in range(2):
+        @pl.when(has[d])
+        def _(d=d):
+            zcopy[d][1].start()
+
+    inner, outer = slice(8, 24), slice(0, 8)
     def mirror(fields, rows):
         for d in range(2):
             @pl.when(jnp.logical_not(has[1 - d]))
@@ -274,13 +304,6 @@
                     return 0
                 lax.fori_loop(*fields, one, 0)
 
-    for d in range(2):
-        @pl.when(has[1 - d])
-        def _(d=d):
-            zcopy[d].wait_recv()
-    inner, outer = slice(0, 16), slice(16, 24)
-    mirror((0, 13), inner)
-
     def pack_y(rows, count):
         slot = iota((count, 128), 1) >> 3
         def one(f, _):
@@ -306,43 +329,43 @@
             return 0
         lax.fori_loop(0, 13, one, 0)
 
-    pack_y(inner, 16)
-    yinner = y_copies(inner, 0)
-    for c in yinner:
-        c.start()
-
     def unpack_x(f):
         for z in range(8):
-            ext[f, 3 + z, 16:19, :] = xr[1, f, pl.ds(z, 3, stride=8), :]
-            ext[f, 3 + z, 21:24, :] = xr[0, f, pl.ds(z, 3, stride=8), :]
+            ext[f, 3 + z, 0:3, :] = xr[1, f, pl.ds(z, 3, stride=8), :]
+            ext[f, 3 + z, 5:8, :] = xr[0, f, pl.ds(z, 3, stride=8), :]
 
     bz, bx, by = [
         jnp.max(jnp.where(live, o & 1, 0).astype(F32), axis=1, keepdims=True) for o in off
     ]
     node, cell = iota((128, 128), 0), iota((128, 128), 1).astype(F32)
     wy = jnp.maximum(0.0, 1.0 - jnp.abs(cell - (2.0 * node.astype(F32) - by)) * 0.5)
-    wy = jnp.where(node <= 64, wy, 0.0).astype(BF16)
+    wy = jnp.where(node < 64, wy, 0.0).astype(BF16)
+    w64 = jnp.maximum(0.0, 1.0 - jnp.abs(iota((1, 128), 1).astype(F32) - (128.0 - by)) * 0.5)
     ci, ki = iota((128, NODES), 0), iota((128, NODES), 1)
     az = (ki * 57) >> 9
     ax = ki - AX * az
     wz = jnp.maximum(0.0, 1.0 - jnp.abs((ci >> 4).astype(F32) - (2.0 * az.astype(F32) - bz)) * 0.5)
     wx = jnp.maximum(0.0, 1.0 - jnp.abs((ci & 15).astype(F32) - (2.0 * ax.astype(F32) - bx)) * 0.5)
-    wzx = (wz * wx).astype(BF16)
+    wzx32 = wz * wx
+    wzx = wzx32.astype(BF16)
 
     grid = gr[me]
     for k in range(1, tiles):
         src = lax.rem(me + tiles - k, tiles)
         remote(gr.at[src], gx.at[src], s_gx.at[k - 1], r_gx.at[src], others[k - 1]).wait_recv()
         grid = grid + gx[src]
-    hi, lo = split(grid)
+    turned = pltpu.roll(grid, 64, 1)
+    column = jnp.sum(wzx32 * turned[23:24, 0:NODES], axis=1, keepdims=True)
+    hi, lo = split(jnp.concatenate([grid, turned], axis=0))
     fine = jnp.dot(jnp.concatenate([hi, lo], axis=0), wy, preferred_element_type=F32)
     fine = fine[0:NODES] + fine[NODES : 2 * NODES]
     hi, lo = split(fine)
     heat = jnp.dot(wzx, hi, preferred_element_type=F32) + jnp.dot(wzx, lo, preferred_element_type=F32)
+    heat = heat + column * w64
     heat = heat.reshape(8, 16, 128)
     heat_out[...] = heat
     for z in range(8):
-        ext[HEAT, 3 + z, 0:16, :] = heat[z]
+        ext[HEAT, 3 + z, 8:24, :] = heat[z]
     for s, first in ((0, 0), (1, 13)):
         for i in range(3):
             xp[s, HEAT, i * 8 : i * 8 + 8, :] = heat[:, first + i, :]
@@ -356,7 +379,7 @@
     for d in range(2):
         a, b = zrows[d]
         zheat.append(remote(
-            ext.at[HEAT, 3 + a : 6 + a, 0:16], ext.at[HEAT, b : b + 3, 0:16], s_zt.at[d], r_zt.at[d], zside[d]
+            ext.at[HEAT, 3 + a : 6 + a, 8:24], ext.at[HEAT, b : b + 3, 8:24], s_zt.at[d], r_zt.at[d], zside[d]
         ))
 
         @pl.when(has[d])
@@ -381,7 +404,7 @@
         for s in range(2):
             n = 2 * d + 1 - s
             xzheat.append(remote(
-                ext.at[HEAT, (3, 10)[d], 8 * s : 8 * s + 8], hxz.at[n], s_hxz.at[2 * d + s], r_hxz.at[n], xz[d][s]
+                ext.at[HEAT, (3, 10)[d], 8 * s + 8 : 8 * s + 16], hxz.at[n], s_hxz.at[2 * d + s], r_hxz.at[n], xz[d][s]
             ))
         for t in range(2):
             n = 2 * d + 1 - t
@@ -392,10 +415,6 @@
             for k in (2 * d, 2 * d + 1):
                 xzheat[k].start()
                 yzheat[k].start()
-
-    for c in yinner:
-        c.wait_recv()
-    unpack_y(inner, 16)
 
     for c in xcopy:
         c.wait_recv()
@@ -431,7 +450,7 @@
                 dcopy[2 * d + s].wait_recv()
             e1, e2 = ((11, 12), (2, 1))[d]
             for s in range(2):
-                x1, x2 = ((23, 22), (16, 17))[s]
+                x1, x2 = ((7, 6), (0, 1))[s]
                 for k, (e, x) in enumerate(((e1, x1), (e2, x1), (e1, x2))):
                     for f in range(13):
                         ext[f, e, x : x + 1, :] = dr[2 * d + s, k, f : f + 1, :]
@@ -440,6 +459,17 @@
     pack_y(outer, 8)
     youter = y_copies(outer, 2)
     for c in youter:
+        c.start()
+
+    for d in range(2):
+        @pl.when(has[1 - d])
+        def _(d=d):
+            for c in zcopy[d]:
+                c.wait_recv()
+    mirror((0, 13), inner)
+    pack_y(inner, 16)
+    yinner = y_copies(inner, 0)
+    for c in yinner:
         c.start()
 
     for c in (*xheat, *yheat):
@@ -479,56 +509,63 @@
     for c in youter:
         c.wait_recv()
     unpack_y(outer, 8)
+    for c in yinner:
+        c.wait_recv()
+    unpack_y(inner, 16)
 
     def step(src, dst, first, last):
+        cells = slice(0, 24)
+
         def sums(r, _):
-            s = src[0, r] * src[0, r]
+            s = src[0, r, cells] * src[0, r, cells]
             for f in range(1, 12):
-                s = s + src[f, r] * src[f, r]
-            u = src[SOL, r]
-            squares[r] = s
-            bend[r] = u - 0.5 * s
-            drives[r] = 60.0 * (1.0 - ext[HEAT, r] - 0.5 * u)
+                s = s + src[f, r, cells] * src[f, r, cells]
+            u = src[SOL, r, cells]
+            squares[r] = 0.1 * s - 0.04
+            bend[r, cells] = u - 0.5 * s
+            drives[r] = 6.0 * (1.0 - ext[HEAT, r, cells] - 0.5 * u)
             return 0
         lax.fori_loop(0, 16, sums, 0)
         final = dst is None
-        n = 16 if final else 24
+        groups = GROUPS[0:2] if final else GROUPS
 
         def fields(f, _):
-            low, high = src[f, LOW], src[f, HIGH]
-            edge = edges(low, high)[0:n]
-            for r in range(first, last):
-                c = src[f, r]
-                around = main_neighbours(src[f, r - 1, 0:n], c, src[f, r + 1, 0:n], edge, r)
-                v = grown(c[0:n], around, squares[r, 0:n], drives[r, 0:n])
-                if final:
-                    grains_out[f, r - 3] = v
-                else:
-                    dst[f, r] = v
-            if not final:
-                for r, c in ((LOW, low), (HIGH, high)):
-                    dst[f, r] = grown(c, strip_neighbours(c), squares[r], drives[r])
+            now = src.at[f]
+            for a, b in groups:
+                edge = edges(now[LOW, a:b, :], now[HIGH, a:b, :])
+                for r in range(first, last):
+                    c, around = main_neighbours(now, r, a, edge)
+                    v = grown(c, around, squares[r, a:b], drives[r, a:b])
+                    if final:
+                        grains_out[f, r - 3, a - 8 : b - 8, :] = v
+                    else:
+                        dst[f, r, a:b, :] = v
+                if not final:
+                    for r in (LOW, HIGH):
+                        c, around = strip_neighbours(now, r, a)
+                        dst[f, r, a:b, :] = grown(c, around, squares[r, a:b], drives[r, a:b])
             return 0
         lax.fori_loop(0, 12, fields, 0)
-        low, high = bend[LOW], bend[HIGH]
-        edge = edges(low, high)[0:n]
-        for r in range(first, last):
-            c = bend[r]
-            lap = main_neighbours(bend[r - 1, 0:n], c, bend[r + 1, 0:n], edge, r) - 6.0 * c[0:n]
-            v = src[SOL, r, 0:n] + 0.15 * lap
-            if final:
-                solute_out[r - 3] = v
-            else:
-                dst[SOL, r] = v
-        if not final:
-            for r, c in ((LOW, low), (HIGH, high)):
-                dst[SOL, r] = src[SOL, r] + 0.15 * (strip_neighbours(c) - 6.0 * c)
+        for a, b in groups:
+            edge = edges(bend[LOW, a:b, :], bend[HIGH, a:b, :])
+            for r in range(first, last):
+                c, around = main_neighbours(bend, r, a, edge)
+                v = src[SOL, r, a:b, :] + 0.15 * (around - 6.0 * c)
+                if final:
+                    solute_out[r - 3, a - 8 : b - 8, :] = v
+                else:
+                    dst[SOL, r, a:b, :] = v
+            if not final:
+                for r in (LOW, HIGH):
+                    c, around = strip_neighbours(bend, r, a)
+                    dst[SOL, r, a:b, :] = src[SOL, r, a:b, :] + 0.15 * (around - 6.0 * c)
 
     step(ext, alt, 1, 13)
     for d in range(2):
         @pl.when(has[d])
         def _(d=d):
-            zcopy[d].wait_send()
+            for c in zcopy[d]:
+                c.wait_send()
 
     step(alt, ext, 2, 12)
     step(ext, None, 3, 11)
@@ -564,9 +601,9 @@
         in_specs=[pl.BlockSpec(memory_space=pltpu.HBM)] * 6,
         out_specs=(vmem,) * 3,
         scratch_shapes=[
-            pltpu.VMEM((NF, 16, 24, 128), F32),
-            pltpu.VMEM((13, 16, 24, 128), F32),
-            pltpu.VMEM((16, 24, 128), F32),
+            pltpu.VMEM((NF, 16, 32, 128), F32),
+            pltpu.VMEM((13, 16, 32, 128), F32),
+            pltpu.VMEM((16, 32, 128), F32),
             pltpu.VMEM((16, 24, 128), F32),
             pltpu.VMEM((16, 24, 128), F32),
             pltpu.VMEM((2, NF, 24, 128), F32),
@@ -588,10 +625,10 @@
             pltpu.VMEM((5, 16, 16, 128), F32),
             pltpu.VMEM((7, 8, 128), F32),
             pltpu.VMEM((NODES, 640), F32),
-            pltpu.VMEM((tiles, NODES, 128), F32),
-            pltpu.VMEM((tiles, NODES, 128), F32),
+            pltpu.VMEM((tiles, 24, 128), F32),
+            pltpu.VMEM((tiles, 24, 128), F32),
             dma((6,)), dma((tiles,)), dma((tiles,)), dma((tiles,)), dma((tiles,)),
-            dma((2,)), dma((2,)), dma((4,)), dma((4,)),
+            dma((4,)), dma((4,)), dma((4,)), dma((4,)),
             dma((2,)), dma((2,)), dma((2,)), dma((2,)),
             dma((4,)), dma((4,)), dma((4,)), dma((4,)),
             dma, dma, dma((2,)), dma((2,)), dma((4,)), dma((4,)),

time: 69 us -> 65.2 us (0.945)
  the two profiles are of different devices: /device:TPU:97 before, /device:TPU:3 now
where the time goes in v3:
time: 65.2 us; the launch traced here: 65 us
  Pallas kernels  60.8 us (93%)
  local copies, waits for them, and re-layouts  3.59 us (6%)
    pallas_call x1, Pallas kernels, body(): pl.pallas_call(functools.partial(kernel, tiles), out_shape=(jax.ShapeDtyp...  60.8 us
    unnamed x7, local copies, waits for them, and re-layouts  3.59 us

profile of v3, /device:TPU:3, one launch (start us, length us, event | category | flops | bytes accessed | tf_op | source)
XLA Modules:
  0.0 65.0 jit_solution(14414599850514889589)
XLA Ops:
  0.6 60.8 %shard_map.85 = (f32[12,8,16,128]{3,2,1,0:T(8,128)}, f32[8,16,128]{2,1,0:T(8,128)}, f32[8,16,128]{2,1,0:T(8,128)}) custom-call(f32[12,8,16,128]{3,2,1,0:T(8,128)} %grains.1, f32[8,16,128]{2,1,0:T(8,128)} %solute.1, f32[40,4096]{1,0:T(8,128)} %bitcast.4, s32[1,20]{1,0:T(1,128)} %bitcast.6, s32[1,20]{1,0:T(1,128)} %bitcast.7, s32[3,1,20]{2,1,0:T(1,128)} %bitcast.5), custom_call_target="tpu_custom_call" | custom-call | tf_op jit(solution)/shard_map/pallas_call | solution.py:594
  61.4 0.0 copy-start.1
  61.4 2.1 %copy.12 = f32[12,8,16,128]{3,2,1,0:T(8,128)} copy(f32[12,8,16,128]{3,2,1,0:T(8,128)} %get-tuple-element.6) | data formatting | bytes 1572864
  63.5 0.0 copy-done.1
  63.5 0.0 copy-start
  63.5 0.6 copy.13
  64.1 0.2 copy-done
  64.4 0.6 copy.14
Async XLA Ops:
  61.4 2.1 %copy-start.1 = (f32[8,16,128]{2,1,0:T(8,128)S(1)}, f32[8,16,128]{2,1,0:T(8,128)}, u32[]{:S(2)}) copy-start(f32[8,16,128]{2,1,0:T(8,128)} %get-tuple-element.7) | copy-start | bytes 196612
  63.5 0.9 %copy-start = (f32[8,16,128]{2,1,0:T(8,128)S(1)}, f32[8,16,128]{2,1,0:T(8,128)}, u32[]{:S(2)}) copy-start(f32[8,16,128]{2,1,0:T(8,128)} %get-tuple-element.8) | copy-start | bytes 196612

commit v4 on v3

--- a/solution.py
+++ b/solution.py
@@ -446,6 +446,17 @@
     for d in range(2):
         @pl.when(has[1 - d])
         def _(d=d):
+            for c in zcopy[d]:
+                c.wait_recv()
+    mirror((0, 13), inner)
+    pack_y(inner, 16)
+    yinner = y_copies(inner, 0)
+    for c in yinner:
+        c.start()
+
+    for d in range(2):
+        @pl.when(has[1 - d])
+        def _(d=d):
             for s in range(2):
                 dcopy[2 * d + s].wait_recv()
             e1, e2 = ((11, 12), (2, 1))[d]
@@ -459,17 +470,6 @@
     pack_y(outer, 8)
     youter = y_copies(outer, 2)
     for c in youter:
-        c.start()
-
-    for d in range(2):
-        @pl.when(has[1 - d])
-        def _(d=d):
-            for c in zcopy[d]:
-                c.wait_recv()
-    mirror((0, 13), inner)
-    pack_y(inner, 16)
-    yinner = y_copies(inner, 0)
-    for c in yinner:
         c.start()
 
     for c in (*xheat, *yheat):
@@ -525,37 +525,42 @@
             bend[r, cells] = u - 0.5 * s
             drives[r] = 6.0 * (1.0 - ext[HEAT, r, cells] - 0.5 * u)
             return 0
-        lax.fori_loop(0, 16, sums, 0)
+        lax.fori_loop(0, 16, sums, 0, unroll=4)
         final = dst is None
-        groups = GROUPS[0:2] if final else GROUPS
+        groups = [(a, b, range(first, last)) for a, b in GROUPS[0:2]]
+        if not final:
+            groups.append((*GROUPS[2], range(first + 1, last - 1)))
+        strips = groups[0 : 3 if first == 1 else 2]
 
         def fields(f, _):
             now = src.at[f]
-            for a, b in groups:
+            for a, b, rows in groups:
                 edge = edges(now[LOW, a:b, :], now[HIGH, a:b, :])
-                for r in range(first, last):
+                for r in rows:
                     c, around = main_neighbours(now, r, a, edge)
                     v = grown(c, around, squares[r, a:b], drives[r, a:b])
                     if final:
                         grains_out[f, r - 3, a - 8 : b - 8, :] = v
                     else:
                         dst[f, r, a:b, :] = v
-                if not final:
+            if not final:
+                for a, b, _ in strips:
                     for r in (LOW, HIGH):
                         c, around = strip_neighbours(now, r, a)
                         dst[f, r, a:b, :] = grown(c, around, squares[r, a:b], drives[r, a:b])
             return 0
         lax.fori_loop(0, 12, fields, 0)
-        for a, b in groups:
+        for a, b, rows in groups:
             edge = edges(bend[LOW, a:b, :], bend[HIGH, a:b, :])
-            for r in range(first, last):
+            for r in rows:
                 c, around = main_neighbours(bend, r, a, edge)
                 v = src[SOL, r, a:b, :] + 0.15 * (around - 6.0 * c)
                 if final:
                     solute_out[r - 3, a - 8 : b - 8, :] = v
                 else:
                     dst[SOL, r, a:b, :] = v
-            if not final:
+        if not final:
+            for a, b, _ in strips:
                 for r in (LOW, HIGH):
                     c, around = strip_neighbours(bend, r, a)
                     dst[SOL, r, a:b, :] = src[SOL, r, a:b, :] + 0.15 * (around - 6.0 * c)
@@ -635,16 +640,19 @@
             dma((4,)), dma((4,)), dma((4,)), dma((4,)),
         ],
         compiler_params=pltpu.CompilerParams(
-            collective_id=0, has_side_effects=True, vmem_limit_bytes=66000000
+            collective_id=0, has_side_effects=True, vmem_limit_bytes=50331648
         ),
-    )(
-        grains,
-        solute,
-        thermal.reshape(thermal.shape[3], thermal.shape[4]),
-        block_slot.reshape(1, -1),
-        block_owner.reshape(1, -1),
-        block_offset.reshape(3, 1, -1),
-    )
+    )(*(
+        pltpu.with_memory_space_constraint(a, pltpu.HBM)
+        for a in (
+            grains,
+            solute,
+            thermal.reshape(thermal.shape[3], thermal.shape[4]),
+            block_slot.reshape(1, -1),
+            block_owner.reshape(1, -1),
+            block_offset.reshape(3, 1, -1),
+        )
+    ))
 
 
 def solution(mesh):

time: 65.2 us -> 60.3 us (0.925)
  Pallas kernels: 60.8 us -> 57.3 us
  local copies, waits for them, and re-layouts: 3.59 us -> 2.14 us
    pallas_call x1, Pallas kernels: 60.8 us -> 57.3 us  [body(): pl.pallas_call(functools.partial(kernel, tiles), out_shape=(jax.ShapeDtyp...]
    unnamed x7 -> x3, local copies, waits for them, and re-layouts: 3.59 us -> 2.14 us
where the time goes in v4:
time: 60.3 us; the launch traced here: 60.1 us
  Pallas kernels  57.3 us (95%)
  local copies, waits for them, and re-layouts  2.14 us (4%)
  between operations  0.64 us (1%)
    pallas_call x1, Pallas kernels, body(): pl.pallas_call(functools.partial(kernel, tiles), out_shape=(jax.ShapeDtyp...  57.3 us
    unnamed x3, local copies, waits for them, and re-layouts  2.14 us

profile of v4, /device:TPU:3, one launch (start us, length us, event | category | flops | bytes accessed | tf_op | source)
XLA Modules:
  0.0 60.1 jit_solution(2960025584956891684)
XLA Ops:
  0.6 57.3 %shard_map.85 = (f32[12,8,16,128]{3,2,1,0:T(8,128)S(1)}, f32[8,16,128]{2,1,0:T(8,128)S(1)}, f32[8,16,128]{2,1,0:T(8,128)S(1)}) custom-call(f32[12,8,16,128]{3,2,1,0:T(8,128)} %grains.1, f32[8,16,128]{2,1,0:T(8,128)} %solute.1, f32[40,4096]{1,0:T(8,128)} %bitcast.4, s32[1,20]{1,0:T(1,128)} %bitcast.6, s32[1,20]{1,0:T(1,128)} %bitcast.7, s32[3,1,20]{2,1,0:T(1,128)} %bitcast.5), custom_call_target="tpu_custom_call" | custom-call | tf_op jit(solution)/shard_map/pallas_call | solution.py:599
  58.0 0.9 %copy.12 = f32[12,8,16,128]{3,2,1,0:T(8,128)} copy(f32[12,8,16,128]{3,2,1,0:T(8,128)S(1)} %get-tuple-element.6) | data formatting | bytes 1572864
  58.9 0.6 %copy.13 = f32[8,16,128]{2,1,0:T(8,128)} copy(f32[8,16,128]{2,1,0:T(8,128)S(1)} %get-tuple-element.7) | data formatting | bytes 131072
  59.5 0.6 %copy.14 = f32[8,16,128]{2,1,0:T(8,128)} copy(f32[8,16,128]{2,1,0:T(8,128)S(1)} %get-tuple-element.8) | data formatting | bytes 131072

commit v5 on v4

--- a/solution.py
+++ b/solution.py
@@ -472,6 +472,35 @@
     for c in youter:
         c.start()
 
+    for c in yinner:
+        c.wait_recv()
+    unpack_y(inner, 16)
+
+    def sums_of(src, r):
+        cells = slice(0, 24)
+        s = src[0, r, cells] * src[0, r, cells]
+        for f in range(1, 12):
+            s = s + src[f, r, cells] * src[f, r, cells]
+        squares[r] = 0.1 * s - 0.04
+        bend[r, cells] = src[SOL, r, cells] - 0.5 * s
+
+    def early_sums(r, _):
+        sums_of(ext, r)
+        return 0
+    lax.fori_loop(0, 14, early_sums, 0, unroll=2)
+    for r in range(3, 11):
+        drives[r, inner] = 6.0 * (1.0 - ext[HEAT, r, inner] - 0.5 * ext[SOL, r, inner])
+
+    def early_fields(f, _):
+        now = ext.at[f]
+        for a, b in GROUPS[0:2]:
+            edge = edges(now[LOW, a:b, :], now[HIGH, a:b, :])
+            for r in range(3, 11):
+                c, around = main_neighbours(now, r, a, edge)
+                alt[f, r, a:b, :] = grown(c, around, squares[r, a:b], drives[r, a:b])
+        return 0
+    lax.fori_loop(0, 12, early_fields, 0)
+
     for c in (*xheat, *yheat):
         c.wait_recv()
     for c in xyheat:
@@ -509,23 +538,21 @@
     for c in youter:
         c.wait_recv()
     unpack_y(outer, 8)
-    for c in yinner:
-        c.wait_recv()
-    unpack_y(inner, 16)
 
     def step(src, dst, first, last):
-        cells = slice(0, 24)
+        def drive(r, _):
+            drives[r] = 6.0 * (1.0 - ext[HEAT, r, 0:24] - 0.5 * src[SOL, r, 0:24])
+            return 0
 
         def sums(r, _):
-            s = src[0, r, cells] * src[0, r, cells]
-            for f in range(1, 12):
-                s = s + src[f, r, cells] * src[f, r, cells]
-            u = src[SOL, r, cells]
-            squares[r] = 0.1 * s - 0.04
-            bend[r, cells] = u - 0.5 * s
-            drives[r] = 6.0 * (1.0 - ext[HEAT, r, cells] - 0.5 * u)
-            return 0
-        lax.fori_loop(0, 16, sums, 0, unroll=4)
+            sums_of(src, r)
+            return drive(r, 0)
+        if first == 1:
+            lax.fori_loop(1, 13, drive, 0, unroll=4)
+        else:
+            lax.fori_loop(first - 1, last + 1, sums, 0, unroll=(last + 2 - first) // 2)
+        for r in (LOW, HIGH):
+            sums(r, 0)
         final = dst is None
         groups = [(a, b, range(first, last)) for a, b in GROUPS[0:2]]
         if not final:
@@ -537,6 +564,8 @@
             for a, b, rows in groups:
                 edge = edges(now[LOW, a:b, :], now[HIGH, a:b, :])
                 for r in rows:
+                    if first == 1 and a and 3 <= r < 11:
+                        continue
                     c, around = main_neighbours(now, r, a, edge)
                     v = grown(c, around, squares[r, a:b], drives[r, a:b])
                     if final:

time: 60.3 us -> 59.8 us (level)
  no operation moved by 1% of the time
where the time goes in v5:
time: 59.8 us; the launch traced here: 59.7 us
  Pallas kernels  56.9 us (95%)
  local copies, waits for them, and re-layouts  2.14 us (4%)
  between operations  0.64 us (1%)
    pallas_call x1, Pallas kernels, body(): pl.pallas_call(functools.partial(kernel, tiles), out_shape=(jax.ShapeDtyp...  56.9 us
    unnamed x3, local copies, waits for them, and re-layouts  2.14 us

profile of v5, /device:TPU:3, one launch (start us, length us, event | category | flops | bytes accessed | tf_op | source)
XLA Modules:
  0.0 59.7 jit_solution(14472864767582816767)
XLA Ops:
  0.6 56.9 %shard_map.85 = (f32[12,8,16,128]{3,2,1,0:T(8,128)S(1)}, f32[8,16,128]{2,1,0:T(8,128)S(1)}, f32[8,16,128]{2,1,0:T(8,128)S(1)}) custom-call(f32[12,8,16,128]{3,2,1,0:T(8,128)} %grains.1, f32[8,16,128]{2,1,0:T(8,128)} %solute.1, f32[40,4096]{1,0:T(8,128)} %bitcast.4, s32[1,20]{1,0:T(1,128)} %bitcast.6, s32[1,20]{1,0:T(1,128)} %bitcast.7, s32[3,1,20]{2,1,0:T(1,128)} %bitcast.5), custom_call_target="tpu_custom_call" | custom-call | tf_op jit(solution)/shard_map/pallas_call | solution.py:628
  57.5 0.9 %copy.12 = f32[12,8,16,128]{3,2,1,0:T(8,128)} copy(f32[12,8,16,128]{3,2,1,0:T(8,128)S(1)} %get-tuple-element.6) | data formatting | bytes 1572864
  58.4 0.6 %copy.13 = f32[8,16,128]{2,1,0:T(8,128)} copy(f32[8,16,128]{2,1,0:T(8,128)S(1)} %get-tuple-element.7) | data formatting | bytes 131072
  59.0 0.6 %copy.14 = f32[8,16,128]{2,1,0:T(8,128)} copy(f32[8,16,128]{2,1,0:T(8,128)S(1)} %get-tuple-element.8) | data formatting | bytes 131072

commit v6 on v5

--- a/solution.py
+++ b/solution.py
@@ -11,7 +11,7 @@
 NF = 14
 SOL = 12
 HEAT = 13
-DIRECT = 4
+DIRECT = 5
 EARLY = 7
 KEY, HZ, HX, HY, LIVE, TILE = range(6)
 AX = 9

time: 59.8 us -> 58.9 us (0.985)
  the two profiles are of different devices: /device:TPU:3 before, /device:TPU:1 now
where the time goes in v6:
time: 58.9 us; the launch traced here: 58.7 us
  Pallas kernels  55.9 us (95%)
  local copies, waits for them, and re-layouts  2.14 us (4%)
  between operations  0.64 us (1%)
    pallas_call x1, Pallas kernels, body(): pl.pallas_call(functools.partial(kernel, tiles), out_shape=(jax.ShapeDtyp...  55.9 us
    unnamed x3, local copies, waits for them, and re-layouts  2.14 us

profile of v6, /device:TPU:1, one launch (start us, length us, event | category | flops | bytes accessed | tf_op | source)
XLA Modules:
  0.0 58.7 jit_solution(3390736132942061315)
XLA Ops:
  0.6 55.9 %shard_map.85 = (f32[12,8,16,128]{3,2,1,0:T(8,128)S(1)}, f32[8,16,128]{2,1,0:T(8,128)S(1)}, f32[8,16,128]{2,1,0:T(8,128)S(1)}) custom-call(f32[12,8,16,128]{3,2,1,0:T(8,128)} %grains.1, f32[8,16,128]{2,1,0:T(8,128)} %solute.1, f32[40,4096]{1,0:T(8,128)} %bitcast.4, s32[1,20]{1,0:T(1,128)} %bitcast.6, s32[1,20]{1,0:T(1,128)} %bitcast.7, s32[3,1,20]{2,1,0:T(1,128)} %bitcast.5), custom_call_target="tpu_custom_call" | custom-call | tf_op jit(solution)/shard_map/pallas_call | solution.py:628
  56.6 0.9 %copy.12 = f32[12,8,16,128]{3,2,1,0:T(8,128)} copy(f32[12,8,16,128]{3,2,1,0:T(8,128)S(1)} %get-tuple-element.6) | data formatting | bytes 1572864
  57.5 0.6 %copy.13 = f32[8,16,128]{2,1,0:T(8,128)} copy(f32[8,16,128]{2,1,0:T(8,128)S(1)} %get-tuple-element.7) | data formatting | bytes 131072
  58.1 0.6 %copy.14 = f32[8,16,128]{2,1,0:T(8,128)} copy(f32[8,16,128]{2,1,0:T(8,128)S(1)} %get-tuple-element.8) | data formatting | bytes 131072
